TPU v7x, 32 devices: a whole 2x2x4 slice. The times are simulated.
32 devices in a mesh: ep: 8 (over z, y), dp: 4 (over x, core).
Axes of the slice: x: 2, y: 2, z: 4, core: 2. Of those that a mesh axis runs over, the one named last changes fastest.
Arguments:
- hidden_in: bfloat16 [49152, 1024], P(('ep', 'dp'))
- topk_idx: int32 [49152, 8], P(('ep', 'dp'))
- grad_out: bfloat16 [49152, 1024], P(('ep', 'dp'))
- norm_gain: float32 [1024], replicated
- w_router: bfloat16 [1024, 32], replicated
- w_gate: bfloat16 [32, 1024, 512], P('ep')
- w_up: bfloat16 [32, 1024, 512], P('ep')
- w_down: bfloat16 [32, 512, 1024], P('ep')
Outputs:
- output 1: bfloat16 [49152, 1024], P(('ep', 'dp'))
- output 2: bfloat16 [49152, 1024], P(('ep', 'dp'))
- output 3: float32 [], replicated
- output 4: float32 [1024], replicated
- output 5: float32 [1024, 32], replicated
- output 6: bfloat16 [32, 1024, 512], P('ep')
- output 7: bfloat16 [32, 1024, 512], P('ep')
- output 8: bfloat16 [32, 512, 1024], P('ep')
All inputs are finite; a program needn't handle non-finite values.
Results may differ from a plain program's by a relative error of at most 0.0108758.
Values are sent between devices in bfloat16 or wider.
A program may use at most 1 GiB of HBM per device.

v0:
```python
import functools
import math
import jax
import jax.numpy as jnp
from jax import lax
from jax.experimental import pallas as pl
from jax.experimental.pallas import tpu as pltpu
from jax.sharding import Mesh, PartitionSpec as P

EPS = 1e-6
ALPHA = 0.001
AUX_SCALE = 0.25
BF = jnp.bfloat16
F32 = jnp.float32
CHUNK = 256
SEG = 128
TILE = 256
LANES = 128
ANY = pl.BlockSpec(memory_space=pl.ANY)


def dot(a, b, dims=((1,), (0,))):
    return lax.dot_general(a, b, (dims, ((), ())), preferred_element_type=F32)


def dispatch_kernel(first, last, experts, cnt, start, end, h_ref, dy_ref, rank_ref, w_ref, *refs):
    n_alias = 0 if first == 0 else 3
    hs, dys, wr, hbuf, dbuf, wbuf, hz, wz, hx, dx, wx, sem, xsem = refs[n_alias:]
    i = pl.program_id(0)
    c = i
    rows = lax.broadcasted_iota(jnp.int32, (SEG, CHUNK), 0)

    def copies(e, at):
        at = pl.multiple_of(at, 16)
        return (
            pltpu.make_async_copy(hbuf.at[e], hs.at[e, pl.ds(at, SEG)], sem.at[0, e]),
            pltpu.make_async_copy(dbuf.at[e], dys.at[e, pl.ds(at, SEG)], sem.at[1, e]),
            pltpu.make_async_copy(wbuf.at[e], wr.at[e, pl.ds(at, SEG)], sem.at[2, e]),
        )

    def select(e, base):
        same = rows + base == rank_ref[pl.ds(e, 1), :]
        pick = jnp.where(same, 1.0, 0.0).astype(BF)
        weight = jnp.sum(jnp.where(same, w_ref[pl.ds(e, 1), :], 0.0), axis=1, keepdims=True)
        return (
            dot(pick, h_ref[...]).astype(BF),
            dot(pick, dy_ref[...]).astype(BF),
            jnp.broadcast_to(weight, (SEG, LANES)),
        )

    def group(q, carry):
        for u in range(4):
            e = q * 4 + u
            h_rows, dy_rows, w_rows = select(e, 0)

            @pl.when(i > 0)
            def _():
                for cp in copies(e, 0):
                    cp.wait()

            hbuf[e] = h_rows
            dbuf[e] = dy_rows
            wbuf[e] = w_rows
            for cp in copies(e, start[c * experts + e]):
                cp.start()
        return carry

    lax.fori_loop(0, experts // 4, group, 0)

    def overflow(e, carry):
        @pl.when(cnt[c * experts + e] > SEG)
        def _():
            h_rows, dy_rows, w_rows = select(e, SEG)
            hx[...] = h_rows
            dx[...] = dy_rows
            wx[...] = w_rows
            at = pl.multiple_of(start[c * experts + e] + SEG, 16)
            extra = (
                pltpu.make_async_copy(hx, hs.at[e, pl.ds(at, SEG)], xsem.at[0]),
                pltpu.make_async_copy(dx, dys.at[e, pl.ds(at, SEG)], xsem.at[1]),
                pltpu.make_async_copy(wx, wr.at[e, pl.ds(at, SEG)], xsem.at[2]),
            )
            for cp in extra:
                cp.start()
            for cp in extra:
                cp.wait()

        return carry

    lax.fori_loop(0, experts, overflow, 0)

    @pl.when(i == pl.num_programs(0) - 1)
    def _():
        def drain(e, carry):
            for cp in copies(e, 0):
                cp.wait()
            return carry

        lax.fori_loop(0, experts, drain, 0)
        if last:
            hz[...] = jnp.zeros_like(hz)
            wz[...] = jnp.zeros_like(wz)

            def tail(e, carry):
                at = pl.multiple_of(end[e], 16)
                zero = (
                    pltpu.make_async_copy(hz, hs.at[e, pl.ds(at, TILE)], xsem.at[0]),
                    pltpu.make_async_copy(hz, dys.at[e, pl.ds(at, TILE)], xsem.at[1]),
                    pltpu.make_async_copy(wz, wr.at[e, pl.ds(at, TILE)], xsem.at[2]),
                )
                for cp in zero:
                    cp.start()
                for cp in zero:
                    cp.wait()
                return carry

            lax.fori_loop(0, experts, tail, 0)


def dispatch(first, last, tables, h, dy, rank_t, w_t, cap, prev=None):
    tok, dim = h.shape
    experts = rank_t.shape[0]
    n = tok // CHUNK
    shapes = (
        jax.ShapeDtypeStruct((experts, cap, dim), BF),
        jax.ShapeDtypeStruct((experts, cap, dim), BF),
        jax.ShapeDtypeStruct((experts, cap, LANES), F32),
    )
    prev = () if prev is None else prev
    return pl.pallas_call(
        functools.partial(dispatch_kernel, first, last, experts),
        out_shape=shapes,
        grid_spec=pltpu.PrefetchScalarGridSpec(
            num_scalar_prefetch=3,
            grid=(n,),
            in_specs=[
                pl.BlockSpec((CHUNK, dim), lambda i, *_: (i, 0)),
                pl.BlockSpec((CHUNK, dim), lambda i, *_: (i, 0)),
                pl.BlockSpec((experts, CHUNK), lambda i, *_: (0, i)),
                pl.BlockSpec((experts, CHUNK), lambda i, *_: (0, i)),
            ] + [ANY] * len(prev),
            out_specs=[ANY] * 3,
            scratch_shapes=[
                pltpu.VMEM((experts, SEG, dim), BF),
                pltpu.VMEM((experts, SEG, dim), BF),
                pltpu.VMEM((experts, SEG, LANES), F32),
                pltpu.VMEM((TILE, dim), BF),
                pltpu.VMEM((TILE, LANES), F32),
                pltpu.VMEM((SEG, dim), BF),
                pltpu.VMEM((SEG, dim), BF),
                pltpu.VMEM((SEG, LANES), F32),
                pltpu.SemaphoreType.DMA((3, experts)),
                pltpu.SemaphoreType.DMA((3,)),
            ],
        ),
        input_output_aliases={7 + k: k for k in range(len(prev))},
        compiler_params=pltpu.CompilerParams(
            dimension_semantics=("arbitrary",), vmem_limit_bytes=40 << 20
        ),
        cost_estimate=pl.CostEstimate(
            flops=4 * n * experts * SEG * CHUNK * dim, bytes_accessed=n * experts * SEG * dim * 4, transcendentals=0
        ),
    )(*tables, h, dy, rank_t, w_t, *prev)


def expert_kernel(tiles, offs, h_ref, dy_ref, wr_ref, *refs):
    pieces, (o_ref, dh_ref, dw_ref, gw_ref, acc) = refs[:4], refs[4:]
    z, i = pl.program_id(0), pl.program_id(1)
    used = tiles[z]
    block = pieces[0].shape[-1]
    halves = range(2)
    parts = range(len(pieces))

    def span(r):
        return pl.ds(pl.multiple_of(offs[r] * block, block), block)

    @pl.when(i == 0)
    def _():
        acc[...] = jnp.zeros_like(acc)

    @pl.when(i < used)
    def _():
        h = [h_ref[0, :, span(r)] for r in parts]
        gate = [sum(dot(h[r], pieces[r][0, f]) for r in parts) for f in halves]
        up = [sum(dot(h[r], pieces[r][0, 2 + f]) for r in parts) for f in halves]
        sig = [jax.nn.sigmoid(v) for v in gate]
        act = [gate[f] * sig[f] for f in halves]
        hidden = [(act[f] * up[f]).astype(BF) for f in halves]
        weight = wr_ref[0][:, :1]
        d_weight = jnp.zeros((h_ref.shape[1], 1), F32)
        d_out = []
        for r in parts:
            out = sum(dot(hidden[f], pieces[r][0, 4 + f]) for f in halves).astype(BF)
            o_ref[0, :, span(r)] = out
            dy_f = dy_ref[0, :, span(r)].astype(F32)
            d_weight = d_weight + jnp.sum(dy_f * out.astype(F32), axis=1, keepdims=True)
            d_out.append((dy_f * weight).astype(BF))
        dw_ref[0] = jnp.broadcast_to(d_weight, dw_ref.shape[1:])
        d_hidden = [sum(dot(d_out[r], pieces[r][0, 4 + f], ((1,), (1,))) for r in parts) for f in halves]
        d_gate = [(d_hidden[f] * up[f] * sig[f] * (1.0 + gate[f] * (1.0 - sig[f]))).astype(BF) for f in halves]
        d_up = [(d_hidden[f] * act[f]).astype(BF) for f in halves]
        for r in parts:
            dh_ref[0, :, span(r)] = sum(
                dot(d_gate[f], pieces[r][0, f], ((1,), (1,))) + dot(d_up[f], pieces[r][0, 2 + f], ((1,), (1,)))
                for f in halves
            ).astype(BF)
        hidden_t = [v.T for v in hidden]
        for r in parts:
            h_t = h[r].T
            for f in halves:
                acc[r, f] += dot(h_t, d_gate[f])
                acc[r, 2 + f] += dot(h_t, d_up[f])
                acc[r, 4 + f] += dot(hidden_t[f], d_out[r])

    @pl.when(i == used)
    def _():
        o_ref[...] = jnp.zeros_like(o_ref)
        dh_ref[...] = jnp.zeros_like(dh_ref)
        dw_ref[...] = jnp.zeros_like(dw_ref)

    @pl.when(i == pl.num_programs(1) - 1)
    def _():
        for r in parts:
            gw_ref[0, offs[r]] = acc[r].astype(BF)


def run_experts(j, n_local, tiles, offs, hs, dys, wr, pieces):
    _, cap, dim = hs.shape
    groups, kinds, depth, _ = pieces[0].shape
    slices = len(pieces)
    steps = cap // TILE
    ff = kinds // 3 * depth

    def row_map(z, i, t, _):
        return (z * n_local + j, jnp.minimum(i, jnp.maximum(t[z] - 1, 0)), 0)

    def out_map(z, i, t, _):
        return (z, jnp.minimum(i, t[z]), 0)

    return pl.pallas_call(
        expert_kernel,
        out_shape=(
            jax.ShapeDtypeStruct((groups, cap, dim), BF),
            jax.ShapeDtypeStruct((groups, cap, dim), BF),
            jax.ShapeDtypeStruct((groups, cap, LANES), F32),
            jax.ShapeDtypeStruct((groups, slices, kinds, depth, depth), BF),
        ),
        grid_spec=pltpu.PrefetchScalarGridSpec(
            num_scalar_prefetch=2,
            grid=(groups, steps),
            in_specs=[
                pl.BlockSpec((1, TILE, dim), row_map),
                pl.BlockSpec((1, TILE, dim), row_map),
                pl.BlockSpec((1, TILE, LANES), row_map),
            ] + [pl.BlockSpec((1, kinds, depth, depth), lambda z, i, *_: (z, 0, 0, 0))] * slices,
            out_specs=[
                pl.BlockSpec((1, TILE, dim), out_map),
                pl.BlockSpec((1, TILE, dim), out_map),
                pl.BlockSpec((1, TILE, LANES), out_map),
                pl.BlockSpec((1, slices, kinds, depth, depth), lambda z, i, *_: (z, 0, 0, 0, 0)),
            ],
            scratch_shapes=[pltpu.VMEM((slices, kinds, depth, depth), F32)],
        ),
        compiler_params=pltpu.CompilerParams(
            dimension_semantics=("arbitrary", "arbitrary"), vmem_limit_bytes=56 << 20
        ),
        cost_estimate=pl.CostEstimate(
            flops=18 * groups * 4 * TILE * dim * ff, bytes_accessed=groups * 4 * TILE * dim * 8, transcendentals=0
        ),
    )(tiles, offs, hs, dys, wr, *pieces)


def combine_kernel(experts, n_local, cnt, start, rank_ref, w_ref, *refs):
    outs, dhs, dws = refs[:n_local], refs[n_local:2 * n_local], refs[2 * n_local:3 * n_local]
    y_ref, dn_ref, dk_ref, obuf, dbuf, kbuf, sel, spread, ox, dx, kx, sem, xsem = refs[3 * n_local:]
    i = pl.program_id(0)
    n = pl.num_programs(0)
    slot = lax.rem(i, 2)
    lane = lax.broadcasted_iota(jnp.int32, (CHUNK, LANES), 1)
    row_lane = lax.broadcasted_iota(jnp.int32, (SEG, LANES), 1)

    def copies(step, s, e):
        z, j = divmod(e, n_local)
        at = pl.multiple_of(start[step * experts + e], 16)
        return (
            pltpu.make_async_copy(outs[j].at[z, pl.ds(at, SEG)], obuf.at[s, pl.ds(e * SEG, SEG)], sem.at[s, 0, e]),
            pltpu.make_async_copy(dhs[j].at[z, pl.ds(at, SEG)], dbuf.at[s, pl.ds(e * SEG, SEG)], sem.at[s, 1, e]),
            pltpu.make_async_copy(dws[j].at[z, pl.ds(at, SEG)], kbuf.at[s, pl.ds(e * SEG, SEG)], sem.at[s, 2, e]),
        )

    @pl.when(i == 0)
    def _():
        for e in range(experts):
            for cp in copies(0, 0, e):
                cp.start()

    @pl.when(i + 1 < n)
    def _():
        for e in range(experts):
            for cp in copies(i + 1, 1 - slot, e):
                cp.start()

    def split(v):
        hi = v.astype(BF).astype(F32)
        mid = (v - hi).astype(BF).astype(F32)
        low = v - hi - mid
        return hi, mid, low

    rank = rank_ref[...]
    w_parts = split(w_ref[...])
    for e in range(experts):
        same = lane == rank[:, e:e + 1]
        at = slice(e * SEG, (e + 1) * SEG)
        sel[0, :, at] = jnp.where(same, 1.0, 0.0).astype(BF)
        for p in range(3):
            sel[1 + p, :, at] = jnp.where(same, w_parts[p][:, e:e + 1], 0.0).astype(BF)

    for e in range(experts):
        for cp in copies(i, slot, e):
            cp.wait()

    def spread_of(e, value):
        parts = split(value)
        out = jnp.where(row_lane == e, parts[0], 0.0)
        out = jnp.where(row_lane == experts + e, parts[1], out)
        return jnp.where(row_lane == 2 * experts + e, parts[2], out).astype(BF)

    for e in range(experts):
        at = pl.ds(e * SEG, SEG)
        spread[at, :] = spread_of(e, kbuf[slot, at, :])
    y_ref[...] = dot(sel[1], obuf[slot]) + dot(sel[2], obuf[slot]) + dot(sel[3], obuf[slot])
    dn_ref[...] = dot(sel[0], dbuf[slot])
    dk_ref[...] = dot(sel[0], spread[...])

    for e in range(experts):
        z, j = divmod(e, n_local)

        @pl.when(cnt[i * experts + e] > SEG)
        def _():
            at = pl.multiple_of(start[i * experts + e] + SEG, 16)
            extra = (
                pltpu.make_async_copy(outs[j].at[z, pl.ds(at, SEG)], ox, xsem.at[0]),
                pltpu.make_async_copy(dhs[j].at[z, pl.ds(at, SEG)], dx, xsem.at[1]),
                pltpu.make_async_copy(dws[j].at[z, pl.ds(at, SEG)], kx, xsem.at[2]),
            )
            for cp in extra:
                cp.start()
            for cp in extra:
                cp.wait()
            same = lane + SEG == rank_ref[:, e:e + 1]
            pick = jnp.where(same, 1.0, 0.0).astype(BF)
            parts = split(w_ref[:, e:e + 1])
            for p in range(3):
                y_ref[...] += dot(jnp.where(same, parts[p], 0.0).astype(BF), ox[...])
            dn_ref[...] += dot(pick, dx[...])
            dk_ref[...] += dot(pick, spread_of(e, kx[...]))


def combine(tables, rank, w, outs, dhs, dws):
    tok = rank.shape[0]
    n_local = len(outs)
    groups, _, dim = outs[0].shape
    experts = groups * n_local
    n = tok // CHUNK
    return pl.pallas_call(
        functools.partial(combine_kernel, experts, n_local),
        out_shape=(
            jax.ShapeDtypeStruct((tok, dim), F32),
            jax.ShapeDtypeStruct((tok, dim), F32),
            jax.ShapeDtypeStruct((tok, LANES), F32),
        ),
        grid_spec=pltpu.PrefetchScalarGridSpec(
            num_scalar_prefetch=2,
            grid=(n,),
            in_specs=[
                pl.BlockSpec((CHUNK, LANES), lambda i, *_: (i, 0)),
                pl.BlockSpec((CHUNK, LANES), lambda i, *_: (i, 0)),
            ] + [ANY] * (3 * n_local),
            out_specs=[
                pl.BlockSpec((CHUNK, dim), lambda i, *_: (i, 0)),
                pl.BlockSpec((CHUNK, dim), lambda i, *_: (i, 0)),
                pl.BlockSpec((CHUNK, LANES), lambda i, *_: (i, 0)),
            ],
            scratch_shapes=[
                pltpu.VMEM((2, experts * SEG, dim), BF),
                pltpu.VMEM((2, experts * SEG, dim), BF),
                pltpu.VMEM((2, experts * SEG, LANES), F32),
                pltpu.VMEM((4, CHUNK, experts * SEG), BF),
                pltpu.VMEM((experts * SEG, LANES), BF),
                pltpu.VMEM((SEG, dim), BF),
                pltpu.VMEM((SEG, dim), BF),
                pltpu.VMEM((SEG, LANES), F32),
                pltpu.SemaphoreType.DMA((2, 3, experts)),
                pltpu.SemaphoreType.DMA((3,)),
            ],
        ),
        compiler_params=pltpu.CompilerParams(
            dimension_semantics=("arbitrary",), vmem_limit_bytes=56 << 20
        ),
        cost_estimate=pl.CostEstimate(
            flops=8 * n * CHUNK * experts * SEG * dim, bytes_accessed=n * experts * SEG * dim * 4, transcendentals=0
        ),
        name="combine",
    )(*tables, rank, w, *outs, *dhs, *dws)


def small_sum_kernel(axes, sizes, whole_ref, split_ref, whole_out, split_out, got_w, got_s, mine, send, recv):
    n = math.prod(sizes)
    me = 0
    for axis, size in zip(axes, sizes):
        me = me * size + lax.axis_index(axis)

    def place(p):
        out = []
        for size in reversed(sizes):
            out.append(lax.rem(p, size))
            p = p // size
        return tuple(reversed(out))

    barrier = pltpu.get_barrier_semaphore()
    for k in range(1, n):
        pl.semaphore_signal(barrier, inc=1, device_id=place(lax.rem(me + k, n)), device_id_type=pl.DeviceIdType.MESH)
    pl.semaphore_wait(barrier, n - 1)

    def copy(src, dst, what, k):
        peer = lax.rem(me + k, n)
        return pltpu.make_async_remote_copy(
            src_ref=src, dst_ref=dst, send_sem=send.at[what, k], recv_sem=recv.at[what, k],
            device_id=place(peer), device_id_type=pl.DeviceIdType.MESH,
        )

    def rows_of(p):
        return split_ref.at[pl.ds(pl.multiple_of(p * 8, 8), 8)]

    first = []
    for k in range(1, n):
        first.append(copy(whole_ref, got_w.at[me], 0, k))
        if split_ref is not None:
            first.append(copy(rows_of(lax.rem(me + k, n)), got_s.at[me], 1, k))
    for cp in first:
        cp.start()
    got_w[me] = whole_ref[...]
    if split_ref is not None:
        got_s[me] = split_ref[pl.ds(pl.multiple_of(me * 8, 8), 8)]
    for cp in first:
        cp.wait()
    whole_out[...] = jnp.sum(got_w[...], axis=0)
    if split_ref is not None:
        mine[...] = jnp.sum(got_s[...], axis=0)
        own = pl.ds(pl.multiple_of(me * 8, 8), 8)
        split_out[own, :] = mine[...]
        second = [copy(mine, split_out.at[own], 2, k) for k in range(1, n)]
        for cp in second:
            cp.start()
        for cp in second:
            cp.wait()


def small_sum(axes, sizes, ident, whole, split=None):
    n = math.prod(sizes)
    vmem = pl.BlockSpec(memory_space=pltpu.VMEM)
    scratch = [pltpu.VMEM((n,) + whole.shape, F32)]
    if split is not None:
        scratch += [pltpu.VMEM((n, 8, LANES), F32), pltpu.VMEM((8, LANES), F32)]
    scratch += [pltpu.SemaphoreType.DMA((3, n)), pltpu.SemaphoreType.DMA((3, n))]
    kernel = functools.partial(small_sum_kernel, axes, sizes)
    if split is None:
        def body(w, wo, gw, ss, rs):
            kernel(w, None, wo, None, gw, None, None, ss, rs)

        args = (whole,)
    else:
        body = kernel
        args = (whole, split)
    out = pl.pallas_call(
        body,
        out_shape=tuple(jax.ShapeDtypeStruct(v.shape, F32) for v in args),
        in_specs=[vmem] * len(args),
        out_specs=tuple([vmem] * len(args)),
        scratch_shapes=scratch,
        compiler_params=pltpu.CompilerParams(collective_id=ident, has_side_effects=True),
    )(*args)
    return out


def assemble_kernel(slices, sizes, offs, *refs):
    groups = len(sizes)
    pieces = [refs[g * slices:(g + 1) * slices] for g in range(groups)]
    gate, up, down, buf, sem_in, sem_out = refs[groups * slices:]
    block = buf.shape[-1]
    base = [sum(sizes[:g]) for g in range(groups)]
    loads = [
        [pltpu.make_async_copy(pieces[g][r], buf.at[r, pl.ds(base[g], sizes[g])], sem_in.at[g, r]) for r in range(slices)]
        for g in range(groups)
    ]
    for g in range(groups):
        for r in range(slices):
            loads[g][r].start()
    stores = []
    for g in range(groups):
        experts = pl.ds(base[g], sizes[g])
        for r in range(slices):
            loads[g][r].wait()
            at = pl.ds(pl.multiple_of(offs[r] * block, block), block)
            for f in range(2):
                part = pl.ds(f * block, block)
                for t, target in enumerate((gate.at[experts, at, part], up.at[experts, at, part], down.at[experts, part, at])):
                    cp = pltpu.make_async_copy(buf.at[r, experts, 2 * t + f], target, sem_out.at[g, r, 2 * t + f])
                    cp.start()
                    stores.append(cp)
    for cp in stores:
        cp.wait()


def assemble(offs, groups, shapes):
    slices = len(groups[0])
    sizes = [g[0].shape[0] for g in groups]
    kinds, depth = groups[0][0].shape[1:3]
    flat = [p for g in groups for p in g]
    return pl.pallas_call(
        functools.partial(assemble_kernel, slices, sizes),
        out_shape=tuple(jax.ShapeDtypeStruct(v, BF) for v in shapes),
        grid_spec=pltpu.PrefetchScalarGridSpec(
            num_scalar_prefetch=1,
            grid=(),
            in_specs=[ANY] * len(flat),
            out_specs=[ANY] * 3,
            scratch_shapes=[
                pltpu.VMEM((slices, sum(sizes), kinds, depth, depth), BF),
                pltpu.SemaphoreType.DMA((len(sizes), slices)),
                pltpu.SemaphoreType.DMA((len(sizes), slices, kinds)),
            ],
        ),
        compiler_params=pltpu.CompilerParams(vmem_limit_bytes=24 << 20),
        name="assemble",
    )(offs, *flat)


def layout_tables(mask):
    tok, experts = mask.shape
    n = tok // CHUNK
    m3 = mask.reshape(n, CHUNK, experts)
    before = jnp.tril(jnp.ones((CHUNK, CHUNK), BF), -1)
    rank = jnp.einsum('ts,cse->cte', before, m3.astype(BF), preferred_element_type=F32)
    rank = jnp.where(m3 > 0, rank, -1.0).astype(jnp.int32).reshape(tok, experts)
    cnt = jnp.sum(m3, axis=1).astype(jnp.int32)
    return rank, cnt


def pad_lanes(v):
    return jnp.pad(v, ((0, 0), (0, LANES - v.shape[1])))


def solution(mesh):
    ep_size = mesh.shape['ep']
    dp_size = mesh.shape['dp']
    n_dev = ep_size * dp_size
    nz, ny = ep_size // 2, 2
    fine = Mesh(mesh.devices.reshape(nz, ny, dp_size), ('z', 'y', 'b'))
    row_spec = P(('z', 'y', 'b'), None)
    exp_spec = P(('z', 'y'), None, None)
    every = ('z', 'y', 'b')
    counts_of = (nz, ny, dp_size)
    swap = [(0, 1), (1, 0)]
    to_x = [(q, q ^ 2) for q in range(dp_size)]
    to_core = [(q, q ^ 1) for q in range(dp_size)]

    def spread_slices(own):
        other_x = lax.ppermute(own, 'b', to_x)
        return (own, lax.ppermute(own, 'b', to_core), other_x, lax.ppermute(other_x, 'b', to_core))

    def block_of(hidden_in, topk_idx, grad_out, norm_gain, w_router, w_gate, w_up, w_down):
        tok, dim = hidden_in.shape
        experts = w_router.shape[1]
        top_k = topk_idx.shape[1]
        n_local, _, ff = w_gate.shape
        tok_total = tok * n_dev
        mine = nz * n_local
        chunks = tok // CHUNK
        per_dev = tok * top_k // experts + tok * top_k // (2 * experts)
        cap = -(-(2 * per_dev + 2 * chunks * 15) // TILE) * TILE + TILE
        depth = dim // dp_size
        y_at = lax.axis_index('y')
        b_at = lax.axis_index('b')
        offs = jnp.bitwise_xor(b_at, jnp.arange(dp_size, dtype=jnp.int32))

        dy_far = lax.ppermute(grad_out, 'y', swap)
        at = b_at * depth

        def blocks(w):
            part = lax.dynamic_slice_in_dim(w, at, depth, 1)
            return part.reshape(n_local, depth, ff // depth, depth).transpose(0, 2, 1, 3)

        d_sl = lax.dynamic_slice_in_dim(w_down, at, depth, 2).reshape(n_local, ff // depth, depth, depth)
        offer = jnp.concatenate([blocks(w_gate), blocks(w_up), d_sl], axis=1)
        pieces = []
        for j in range(n_local):
            gathered = lax.all_gather(offer[j], 'z')
            pieces.append(spread_slices(gathered))

        x_f = hidden_in.astype(F32)
        inv_rms = lax.rsqrt(jnp.mean(x_f * x_f, axis=-1, keepdims=True) + EPS)
        normed = (x_f * inv_rms * norm_gain).astype(BF)
        h_far = lax.ppermute(normed, 'y', swap)
        logits = jnp.dot(normed, w_router, preferred_element_type=F32)
        probs = jax.nn.softmax(logits, axis=-1)
        eye = jnp.arange(experts, dtype=jnp.int32)
        mask = jnp.zeros((tok, experts), F32)
        for k in range(top_k):
            mask = mask + (topk_idx[:, k:k + 1] == eye[None, :]).astype(F32)
        chosen = mask * probs
        chosen_sum = jnp.sum(chosen, axis=1, keepdims=True)
        weights = chosen / chosen_sum

        def halves(v):
            v4 = v.reshape(tok, nz, ny, n_local)
            a, b = v4[:, :, 0].reshape(tok, mine), v4[:, :, 1].reshape(tok, mine)
            own = jnp.where(y_at == 0, a, b)
            return own, jnp.where(y_at == 0, b, a)

        m_near, m_send = halves(mask)
        w_near, w_send = halves(weights)
        far = lax.ppermute(jnp.concatenate([m_send, w_send], axis=1), 'y', swap)
        m_far, w_far = far[:, :mine], far[:, mine:]

        rank_near, cnt_near = layout_tables(m_near)
        pad_near = (cnt_near + 15) // 16 * 16
        end_near = jnp.cumsum(pad_near, axis=0)
        near = (cnt_near.reshape(-1), (end_near - pad_near).reshape(-1), end_near[-1])
        rank_far, cnt_far = layout_tables(m_far)
        pad_far = (cnt_far + 15) // 16 * 16
        end_far = jnp.cumsum(pad_far, axis=0) + end_near[-1]
        end = end_far[-1]
        far_t = (cnt_far.reshape(-1), (end_far - pad_far).reshape(-1), end)
        used = ((end + TILE - 1) // TILE).reshape(nz, n_local)

        rows = dispatch(0, False, near, normed, grad_out, rank_near.T, w_near.T, cap)
        rows = dispatch(1, True, far_t, h_far, dy_far, rank_far.T, w_far.T, cap, rows)

        stats_in = jnp.pad(jnp.stack([jnp.sum(mask, axis=0), jnp.sum(probs, axis=0)]), ((0, 6), (0, LANES - experts)))
        stats_in, marks = lax.optimization_barrier((stats_in, rows[2]))
        (stats,) = small_sum(every, counts_of, 0, stats_in)
        used, stats = lax.optimization_barrier((used, stats))
        rows = (rows[0], rows[1], marks)
        load_frac = stats[0, :experts] / (top_k * tok_total)
        aux_loss = ALPHA * experts * jnp.sum(load_frac * stats[1, :experts] / tok_total)

        outs, dhs, dws, sums = [], [], [], []
        for j in range(n_local):
            o, dh, dw, gw = run_experts(j, n_local, used[:, j], offs, *rows, pieces[j])
            used, dw = lax.optimization_barrier((used, dw))
            outs.append(o)
            dhs.append(dh)
            dws.append(dw)
            sums.append(lax.psum_scatter(gw.reshape((nz * dp_size,) + gw.shape[2:]), ('z', 'b'), scatter_dimension=0))

        def total(v):
            return v[:, :mine] + v[:, mine:2 * mine] + v[:, 2 * mine:3 * mine]

        y_far, dn_far, dk_far = combine(far_t[:2], pad_lanes(rank_far), pad_lanes(w_far), outs, dhs, dws)
        dk_back = lax.ppermute(total(dk_far), 'y', swap)
        y_back = lax.ppermute(y_far, 'y', swap)
        dn_back = lax.ppermute(dn_far, 'y', swap)
        y_near, dn_near, dk_near = combine(near[:2], pad_lanes(rank_near), pad_lanes(w_near), outs, dhs, dws)

        *early, y_near = lax.optimization_barrier((*sums[:-1], y_near))
        late, y_near = lax.optimization_barrier((sums[-1], y_near))
        grads = assemble(
            offs,
            [spread_slices(jnp.stack(early)), spread_slices(late[None])],
            (w_gate.shape, w_up.shape, w_down.shape),
        )
        block_out = (x_f + (y_near + y_back)).astype(BF)

        near4 = total(dk_near).reshape(tok, nz, n_local)
        back4 = dk_back.reshape(tok, nz, n_local)
        d_weight = jnp.stack([jnp.where(y_at == 0, near4, back4), jnp.where(y_at == 0, back4, near4)], axis=2).reshape(tok, experts)
        d_chosen = (d_weight - jnp.sum(weights * d_weight, axis=1, keepdims=True)) / chosen_sum
        aux_coef = AUX_SCALE * math.sqrt(dim * experts) * experts
        d_prob = mask * d_chosen + aux_coef * load_frac[None, :]
        d_logit = probs * (d_prob - jnp.sum(probs * d_prob, axis=1, keepdims=True))
        d_logit_bf = d_logit.astype(BF)
        router_part = jnp.einsum('td,te->de', normed, d_logit_bf, preferred_element_type=F32)
        d_normed = dn_near + dn_back + jnp.einsum('te,de->td', d_logit_bf, w_router, preferred_element_type=F32)
        gain_part = jnp.sum(d_normed * x_f * inv_rms, axis=0)
        d_scaled = d_normed * norm_gain
        inv_cube = inv_rms * inv_rms * inv_rms
        grad_in = (grad_out.astype(F32) + inv_rms * d_scaled - x_f * inv_cube * jnp.mean(d_scaled * x_f, axis=-1, keepdims=True)).astype(BF)
        gain_sum, router_sum = small_sum(
            every, counts_of, 1, gain_part.reshape(-1, LANES), router_part.reshape(-1, LANES)
        )
        return (block_out, grad_in, aux_loss, gain_sum.reshape(dim), router_sum.reshape(dim, experts), *grads)


    return jax.shard_map(
        block_of,
        mesh=fine,
        in_specs=(row_spec, row_spec, row_spec, P(None), P(None, None), exp_spec, exp_spec, exp_spec),
        out_specs=(row_spec, row_spec, P(), P(None), P(None, None), exp_spec, exp_spec, exp_spec),
        check_vma=False,
    )
```

profile of v0, /device:TPU:14, one launch (start us, length us, event | category | flops | bytes accessed | tf_op | source)
XLA Modules:
  0.0 1239.2 jit_solution(6943025878876368733)
XLA Ops:
  15.8 2.4 copy.103
  18.3 2.3 copy.104
  20.7 2.3 copy.105
  28.9 51.9 %all-gather.5.cloned.1.call-done.refs_0_ = bf16[4,6,256,256]{3,2,1,0:T(8,128)(2,1)} async-done(((bf16[1,6,256,256]{3,2,1,0:T(8,128)(2,1)}), bf16[4,6,256,256]{3,2,1,0:T(8,128)(2,1)}) %all-gather.5.cloned.1.call-update) | async-done | bytes 3145744 | tf_op jit(solution)/shard_map/all_gather | solution.py:598
  88.6 2.3 copy.106
  95.1 2.0 copy.96
  98.5 2.0 copy-done.1
  100.5 35.8 %shard_map.143 = (bf16[16,1792,1024]{2,1,0:T(8,128)(2,1)}, bf16[16,1792,1024]{2,1,0:T(8,128)(2,1)}, f32[16,1792,128]{2,1,0:T(8,128)}) custom-call(s32[96]{0:T(128)S(1)} %convert_element_type.122.cnt, s32[96]{0:T(128)S(1)} %multiply_subtract_fusion.start, s32[16]{0:T(128)S(1)} %slice_reduce_fusion.end, bf16[1536,1024]{1,0:T(8,128)(2,1)S(1)} %fusion.2.h_ref, ...), custom_call_target="tpu_custom_call" | custom-call | flops 12884901888 | bytes 50331648 | tf_op jit(solution)/shard_map/pallas_call | solution.py:130
  136.4 14.3 %collective-permute-done.4.refs_2_ = bf16[4,6,256,256]{3,2,1,0:T(8,128)(2,1)} collective-permute-done((bf16[4,6,256,256]{3,2,1,0:T(8,128)(2,1)}, bf16[4,6,256,256]{3,2,1,0:T(8,128)(2,1)}, u32[]{:S(2)}, u32[]{:S(2)}) %collective-permute-start.4) | collective-permute-done | bytes 3145760 | tf_op jit(solution)/shard_map/ppermute | solution.py:569
  159.1 8.3 collective-permute-done.2.dy_ref
  167.4 53.8 %shard_map.144 = (bf16[16,1792,1024]{2,1,0:T(8,128)(2,1)}, bf16[16,1792,1024]{2,1,0:T(8,128)(2,1)}, f32[16,1792,128]{2,1,0:T(8,128)}) custom-call(s32[96]{0:T(128)S(1)} %convert_element_type.119.cnt, s32[96]{0:T(128)S(1)} %multiply_subtract_fusion.1.start, s32[16]{0:T(128)S(1)} %get-tuple-element.153.end, ...), custom_call_target="tpu_custom_call", output_to_operand_aliasing={{0}: (7, {}), {1}: (8, {}), {2}: (9, {})} | custom-call | flops 12884901888 | bytes 50331648 | tf_op jit(solution)/shard_map/pallas_call | solution.py:130
  221.2 14.7 %shard_map.145 = f32[8,128]{1,0:T(8,128)} custom-call(f32[8,128]{1,0:T(8,128)} %select_maximum_fusion.w), custom_call_target="tpu_custom_call" | custom-call | tf_op jit(solution)/shard_map/pallas_call | solution.py:475
  236.5 76.4 %shard_map.146 = (bf16[4,1792,1024]{2,1,0:T(8,128)(2,1)}, bf16[4,1792,1024]{2,1,0:T(8,128)(2,1)}, f32[4,1792,128]{2,1,0:T(8,128)}, bf16[4,4,6,256,256]{4,3,2,1,0:T(8,128)(2,1)}) custom-call(s32[4]{0:T(128)} %slice_reduce_fusion.13.tiles, s32[4]{0:T(128)} %iota_xor_fusion.offs, bf16[16,1792,1024]{2,1,0:T(8,128)(2,1)} %get-tuple-element.64.h_ref, ...), custom_call_target="tpu_custom_call" | custom-call | flops 38654705664 | bytes 33554432 | tf_op jit(solution)/shard_map/pallas_call | solution.py:240
  313.9 3.2 collective-permute-start.6
  317.1 82.9 %collective-permute-done.7.refs_2_ = bf16[4,6,256,256]{3,2,1,0:T(8,128)(2,1)S(1)} collective-permute-done((bf16[4,6,256,256]{3,2,1,0:T(8,128)(2,1)}, bf16[4,6,256,256]{3,2,1,0:T(8,128)(2,1)S(1)}, u32[]{:S(2)}, u32[]{:S(2)}) %collective-permute-start.7) | collective-permute-done | bytes 3145760 | tf_op jit(solution)/shard_map/ppermute | solution.py:569
  399.9 1.9 collective-permute-start.8
  402.5 4.7 collective-permute-done.8.refs_3_
  407.2 76.6 %shard_map.147 = (bf16[4,1792,1024]{2,1,0:T(8,128)(2,1)}, bf16[4,1792,1024]{2,1,0:T(8,128)(2,1)}, f32[4,1792,128]{2,1,0:T(8,128)}, bf16[4,4,6,256,256]{4,3,2,1,0:T(8,128)(2,1)}) custom-call(s32[4]{0:T(128)} %slice_reduce_fusion.12.tiles, s32[4]{0:T(128)} %iota_xor_fusion.offs, bf16[16,1792,1024]{2,1,0:T(8,128)(2,1)} %get-tuple-element.64.h_ref, ...), custom_call_target="tpu_custom_call" | custom-call | flops 38654705664 | bytes 33554432 | tf_op jit(solution)/shard_map/pallas_call | solution.py:240
  484.4 91.7 %collective-permute-done.10.refs_2_ = bf16[4,6,256,256]{3,2,1,0:T(8,128)(2,1)S(1)} collective-permute-done((bf16[4,6,256,256]{3,2,1,0:T(8,128)(2,1)}, bf16[4,6,256,256]{3,2,1,0:T(8,128)(2,1)S(1)}, u32[]{:S(2)}, u32[]{:S(2)}) %collective-permute-start.10) | collective-permute-done | bytes 3145760 | tf_op jit(solution)/shard_map/ppermute | solution.py:569
  577.0 4.9 collective-permute-done.11.refs_3_
  581.9 76.5 %shard_map.148 = (bf16[4,1792,1024]{2,1,0:T(8,128)(2,1)}, bf16[4,1792,1024]{2,1,0:T(8,128)(2,1)}, f32[4,1792,128]{2,1,0:T(8,128)}, bf16[4,4,6,256,256]{4,3,2,1,0:T(8,128)(2,1)}) custom-call(s32[4]{0:T(128)} %slice_reduce_fusion.11.tiles, s32[4]{0:T(128)} %iota_xor_fusion.offs, bf16[16,1792,1024]{2,1,0:T(8,128)(2,1)} %get-tuple-element.64.h_ref, ...), custom_call_target="tpu_custom_call" | custom-call | flops 38654705664 | bytes 33554432 | tf_op jit(solution)/shard_map/pallas_call | solution.py:240
  658.9 92.5 %collective-permute-done.13.refs_2_ = bf16[4,6,256,256]{3,2,1,0:T(8,128)(2,1)S(1)} collective-permute-done((bf16[4,6,256,256]{3,2,1,0:T(8,128)(2,1)}, bf16[4,6,256,256]{3,2,1,0:T(8,128)(2,1)S(1)}, u32[]{:S(2)}, u32[]{:S(2)}) %collective-permute-start.13) | collective-permute-done | bytes 3145760 | tf_op jit(solution)/shard_map/ppermute | solution.py:569
  752.3 4.9 collective-permute-done.14.refs_3_
  757.2 57.4 %shard_map.149 = (bf16[4,1792,1024]{2,1,0:T(8,128)(2,1)}, bf16[4,1792,1024]{2,1,0:T(8,128)(2,1)}, f32[4,1792,128]{2,1,0:T(8,128)}, bf16[4,4,6,256,256]{4,3,2,1,0:T(8,128)(2,1)}) custom-call(s32[4]{0:T(128)} %slice_reduce_fusion.10.tiles, s32[4]{0:T(128)} %iota_xor_fusion.offs, bf16[16,1792,1024]{2,1,0:T(8,128)(2,1)} %get-tuple-element.64.h_ref, ...), custom_call_target="tpu_custom_call" | custom-call | flops 38654705664 | bytes 33554432 | tf_op jit(solution)/shard_map/pallas_call | solution.py:240
  816.6 2.1 pad.22.w_ref
  818.7 2.1 pad.21.rank_ref
  820.7 47.8 %combine.3 = (f32[1536,1024]{1,0:T(8,128)}, f32[1536,1024]{1,0:T(8,128)}, f32[1536,128]{1,0:T(8,128)}) custom-call(s32[96]{0:T(128)} %copy-done.5, s32[96]{0:T(128)} %copy-done.7, s32[1536,128]{1,0:T(8,128)} %pad.21.rank_ref, f32[1536,128]{1,0:T(8,128)} %pad.22.w_ref, bf16[4,1792,1024]{2,1,0:T(8,128)(2,1)} %get-tuple-element.77.refs_0_, ...), custom_call_target="tpu_custom_call" | custom-call | flops 25769803776 | bytes 50331648 | tf_op jit(solution)/shard_map/combine/pallas_call | solution.py:365
  869.8 2.1 pad.19.rank_ref
  871.9 2.1 pad.20.w_ref
  874.0 2.0 collective-permute-start.15
  876.0 46.6 %combine.2 = (f32[1536,1024]{1,0:T(8,128)}, f32[1536,1024]{1,0:T(8,128)}, f32[1536,128]{1,0:T(8,128)}) custom-call(s32[96]{0:T(128)} %copy-done.6, s32[96]{0:T(128)} %copy-done.8, s32[1536,128]{1,0:T(8,128)} %pad.19.rank_ref, f32[1536,128]{1,0:T(8,128)} %pad.20.w_ref, bf16[4,1792,1024]{2,1,0:T(8,128)(2,1)} %get-tuple-element.77.refs_0_, ...), custom_call_target="tpu_custom_call" | custom-call | flops 25769803776 | bytes 50331648 | tf_op jit(solution)/shard_map/combine/pallas_call | solution.py:365
  922.7 3.4 pad_maximum_fusion.1.refs_0_
  926.1 3.6 collective-permute-start.19
  934.5 207.0 %collective-permute-done.17 = f32[1536,16]{0,1:T(8,128)S(1)} collective-permute-done((f32[1536,16]{0,1:T(8,128)S(1)}, f32[1536,16]{0,1:T(8,128)S(1)}, u32[]{:S(2)}, u32[]{:S(2)}) %collective-permute-start.17) | collective-permute-done | bytes 98336 | tf_op jit(solution)/shard_map/ppermute | solution.py:661
  1142.7 3.6 broadcast_select_fusion.1
  1146.3 2.0 copy.110
  1149.9 2.0 copy.112
  1159.2 2.9 fusion.45
  1162.1 1.9 reshape.251.split_ref
  1164.0 4.6 fusion.46
  1168.6 2.5 collective-permute-start.18
  1171.1 3.1 collective-permute-start.22
  1174.5 12.3 fusion.9
  1186.8 18.1 %shard_map.150 = (f32[8,128]{1,0:T(8,128)}, f32[256,128]{1,0:T(8,128)}) custom-call(f32[8,128]{1,0:T(8,128)} %bitcast.105, f32[256,128]{1,0:T(8,128)} %reshape.251.split_ref), custom_call_target="tpu_custom_call" | custom-call | tf_op jit(solution)/shard_map/pallas_call | solution.py:475
  1204.9 1.9 reshape.253
  1206.7 1.9 copy.115
  1209.2 11.5 fusion.6
  1220.7 9.7 assemble.1
  (225 shorter events, 60.0 us)
Async XLA Ops:
  7.2 19.2 %copy-start = (bf16[1024,32]{0,1:T(8,128)(2,1)S(1)}, bf16[1024,32]{0,1:T(8,128)(2,1)}, u32[]{:S(2)}) copy-start(bf16[1024,32]{0,1:T(8,128)(2,1)} %param.12) | copy-start | bytes 196612
  7.2 73.6 %all-gather.5.cloned.1.call-start = ((), (), s32[]{:S(2)}) async-start(), calls=%async_computation.4 | async-start | bytes 3932160 | tf_op jit(solution)/shard_map/all_gather | solution.py:598
  18.3 294.9 %all-gather.7.cloned.1.call-start = ((), (), s32[]{:S(2)}) async-start(), calls=%async_computation.5 | async-start | bytes 3932160 | tf_op jit(solution)/shard_map/all_gather | solution.py:598
  20.7 463.3 %all-gather.9.cloned.1.call-start = ((), (), s32[]{:S(2)}) async-start(), calls=%async_computation.6 | async-start | bytes 3932160 | tf_op jit(solution)/shard_map/all_gather | solution.py:598
  23.0 635.5 %all-gather.11.cloned.1.call-start = ((), (), s32[]{:S(2)}) async-start(), calls=%async_computation.7 | async-start | bytes 3932160 | tf_op jit(solution)/shard_map/all_gather | solution.py:598
  25.8 133.3 %collective-permute-start.1 = (bf16[1536,1024]{1,0:T(8,128)(2,1)S(1)}, bf16[1536,1024]{1,0:T(8,128)(2,1)}, u32[]{:S(2)}, u32[]{:S(2)}) collective-permute-start(bf16[1536,1024]{1,0:T(8,128)(2,1)S(1)} %fusion.2.h_ref), channel_id=1, source_target_pairs={{0,4},{4,0},{1,5},{5,1},{2,6},{6,2},{3,7},{7,3},{8,12},{12,8},{9,1... | collective-permute-start | bytes 9437192 | tf_op jit(solution)/shard_map/ppermute | solution.py:604
  27.7 63.7 %copy-start.19 = (s32[1536]{0:T(1024)}, s32[1536]{0:T(1024)S(1)}, u32[]{:S(2)}) copy-start(s32[1536]{0:T(1024)S(1)} %get-tuple-element.145) | copy-start | bytes 18436
  27.7 63.7 %copy-start.21 = (s32[1536]{0:T(1024)}, s32[1536]{0:T(1024)S(1)}, u32[]{:S(2)}) copy-start(s32[1536]{0:T(1024)S(1)} %get-tuple-element.146) | copy-start | bytes 18436
  27.7 63.7 %copy-start.23 = (s32[1536]{0:T(1024)}, s32[1536]{0:T(1024)S(1)}, u32[]{:S(2)}) copy-start(s32[1536]{0:T(1024)S(1)} %get-tuple-element.147) | copy-start | bytes 18436
  27.7 63.7 %copy-start.25 = (s32[1536]{0:T(1024)}, s32[1536]{0:T(1024)S(1)}, u32[]{:S(2)}) copy-start(s32[1536]{0:T(1024)S(1)} %get-tuple-element.148) | copy-start | bytes 18436
  27.7 63.7 %copy-start.27 = (s32[1536]{0:T(1024)}, s32[1536]{0:T(1024)S(1)}, u32[]{:S(2)}) copy-start(s32[1536]{0:T(1024)S(1)} %get-tuple-element.149) | copy-start | bytes 18436
  27.7 69.4 %copy-start.29 = (s32[1536]{0:T(1024)}, s32[1536]{0:T(1024)S(1)}, u32[]{:S(2)}) copy-start(s32[1536]{0:T(1024)S(1)} %get-tuple-element.150) | copy-start | bytes 18436
  27.7 69.4 %copy-start.31 = (s32[1536]{0:T(1024)}, s32[1536]{0:T(1024)S(1)}, u32[]{:S(2)}) copy-start(s32[1536]{0:T(1024)S(1)} %get-tuple-element.151) | copy-start | bytes 18436
  27.7 69.4 %copy-start.33 = (s32[1536]{0:T(1024)}, s32[1536]{0:T(1024)S(1)}, u32[]{:S(2)}) copy-start(s32[1536]{0:T(1024)S(1)} %get-tuple-element.152) | copy-start | bytes 18436
  80.8 69.8 %collective-permute-start.4 = (bf16[4,6,256,256]{3,2,1,0:T(8,128)(2,1)}, bf16[4,6,256,256]{3,2,1,0:T(8,128)(2,1)}, u32[]{:S(2)}, u32[]{:S(2)}) collective-permute-start(bf16[4,6,256,256]{3,2,1,0:T(8,128)(2,1)} %all-gather.5.cloned.1.call-done.refs_0_), channel_id=1, source_target_pairs={{0,2},{1,3},{2,0},{3,1},{4,6},{5,7},{6,4},{7,5},{8,10},{9,11},{10,... | collective-permute-start | bytes 9437192 | tf_op jit(solution)/shard_map/ppermute | solution.py:569
  86.6 65.2 %collective-permute-start = (f32[1536,32]{0,1:T(8,128)}, f32[1536,32]{0,1:T(8,128)}, u32[]{:S(2)}, u32[]{:S(2)}) collective-permute-start(f32[1536,32]{0,1:T(8,128)} %pad_maximum_fusion.2), channel_id=1, source_target_pairs={{0,4},{4,0},{1,5},{5,1},{2,6},{6,2},{3,7},{7,3},{8,12},{12,8},{9,1... | collective-permute-start | bytes 589832 | tf_op jit(solution)/shard_map/ppermute | solution.py:623
  87.1 80.3 %collective-permute-start.2 = (bf16[1536,1024]{1,0:T(8,128)(2,1)}, bf16[1536,1024]{1,0:T(8,128)(2,1)}, u32[]{:S(2)}, u32[]{:S(2)}) collective-permute-start(bf16[1536,1024]{1,0:T(8,128)(2,1)} %dy_ref.1), channel_id=1, source_target_pairs={{0,4},{4,0},{1,5},{5,1},{2,6},{6,2},{3,7},{7,3},{8,12},{12,8},{9,1... | collective-permute-start | bytes 9437192 | tf_op jit(solution)/shard_map/ppermute | solution.py:587
  90.9 831.8 %reduce-scatter.7.cloned.1.call-start = ((), (), s32[]{:S(2)}) async-start(), calls=%async_computation.9 | async-start | bytes 13369344 | tf_op jit(solution)/shard_map/reduce_scatter | solution.py:655
  92.9 43.4 %copy-start.6 = (s32[96]{0:T(128)}, s32[96]{0:T(128)S(1)}, u32[]{:S(2)}) copy-start(s32[96]{0:T(128)S(1)} %convert_element_type.122.cnt) | copy-start | bytes 1156
  93.1 43.2 %copy-start.8 = (s32[96]{0:T(128)}, s32[96]{0:T(128)S(1)}, u32[]{:S(2)}) copy-start(s32[96]{0:T(128)S(1)} %multiply_subtract_fusion.start) | copy-start | bytes 1156
  136.3 100.2 %collective-permute-start.3 = (bf16[4,6,256,256]{3,2,1,0:T(8,128)(2,1)}, bf16[4,6,256,256]{3,2,1,0:T(8,128)(2,1)}, u32[]{:S(2)}, u32[]{:S(2)}) collective-permute-start(bf16[4,6,256,256]{3,2,1,0:T(8,128)(2,1)} %all-gather.5.cloned.1.call-done.refs_0_), channel_id=1, source_target_pairs={{0,1},{1,0},{2,3},{3,2},{4,5},{5,4},{6,7},{7,6},{8,9},{9,8},{10,11... | collective-permute-start | bytes 9437192 | tf_op jit(solution)/shard_map/ppermute | solution.py:570
  150.6 85.9 %collective-permute-start.5 = (bf16[4,6,256,256]{3,2,1,0:T(8,128)(2,1)}, bf16[4,6,256,256]{3,2,1,0:T(8,128)(2,1)}, u32[]{:S(2)}, u32[]{:S(2)}) collective-permute-start(bf16[4,6,256,256]{3,2,1,0:T(8,128)(2,1)} %collective-permute-done.4.refs_2_), channel_id=1, source_target_pairs={{0,1},{1,0},{2,3},{3,2},{4,5},{5,4},{6,7},{7,6},{8,9},{9,8},{10,11... | collective-permute-start | bytes 9437192 | tf_op jit(solution)/shard_map/ppermute | solution.py:570
  154.6 66.6 %copy-start.5 = (s32[96]{0:T(128)}, s32[96]{0:T(128)S(1)}, u32[]{:S(2)}) copy-start(s32[96]{0:T(128)S(1)} %convert_element_type.119.cnt) | copy-start | bytes 1156
  159.1 62.1 %copy-start.7 = (s32[96]{0:T(128)}, s32[96]{0:T(128)S(1)}, u32[]{:S(2)}) copy-start(s32[96]{0:T(128)S(1)} %multiply_subtract_fusion.1.start) | copy-start | bytes 1156
  313.0 609.7 %reduce-scatter.9.cloned.1.call-start = ((), (), s32[]{:S(2)}) async-start(), calls=%async_computation.10 | async-start | bytes 13369344 | tf_op jit(solution)/shard_map/reduce_scatter | solution.py:655
  313.2 86.7 %collective-permute-start.7 = (bf16[4,6,256,256]{3,2,1,0:T(8,128)(2,1)}, bf16[4,6,256,256]{3,2,1,0:T(8,128)(2,1)S(1)}, u32[]{:S(2)}, u32[]{:S(2)}) collective-permute-start(bf16[4,6,256,256]{3,2,1,0:T(8,128)(2,1)} %all-gather.7.cloned.1.call-done.refs_0_), channel_id=1, source_target_pairs={{0,2},{1,3},{2,0},{3,1},{4,6},{5,7},{6,4},{7,5},{8,10},{9,11},{10,... | collective-permute-start | bytes 9437192 | tf_op jit(solution)/shard_map/ppermute | solution.py:569
  313.9 88.6 %collective-permute-start.6 = (bf16[4,6,256,256]{3,2,1,0:T(8,128)(2,1)}, bf16[4,6,256,256]{3,2,1,0:T(8,128)(2,1)}, u32[]{:S(2)}, u32[]{:S(2)}) collective-permute-start(bf16[4,6,256,256]{3,2,1,0:T(8,128)(2,1)} %all-gather.7.cloned.1.call-done.refs_0_), channel_id=1, source_target_pairs={{0,1},{1,0},{2,3},{3,2},{4,5},{5,4},{6,7},{7,6},{8,9},{9,8},{10,11... | collective-permute-start | bytes 9437192 | tf_op jit(solution)/shard_map/ppermute | solution.py:570
  399.9 7.3 collective-permute-start.8
  483.9 438.8 %reduce-scatter.11.cloned.1.call-start = ((), (), s32[]{:S(2)}) async-start(), calls=%async_computation.11 | async-start | bytes 13369344 | tf_op jit(solution)/shard_map/reduce_scatter | solution.py:655
  484.0 92.1 %collective-permute-start.10 = (bf16[4,6,256,256]{3,2,1,0:T(8,128)(2,1)}, bf16[4,6,256,256]{3,2,1,0:T(8,128)(2,1)S(1)}, u32[]{:S(2)}, u32[]{:S(2)}) collective-permute-start(bf16[4,6,256,256]{3,2,1,0:T(8,128)(2,1)} %all-gather.9.cloned.1.call-done.refs_0_), channel_id=1, source_target_pairs={{0,2},{1,3},{2,0},{3,1},{4,6},{5,7},{6,4},{7,5},{8,10},{9,11},{10,... | collective-permute-start | bytes 9437192 | tf_op jit(solution)/shard_map/ppermute | solution.py:569
  484.2 92.8 %collective-permute-start.9 = (bf16[4,6,256,256]{3,2,1,0:T(8,128)(2,1)}, bf16[4,6,256,256]{3,2,1,0:T(8,128)(2,1)}, u32[]{:S(2)}, u32[]{:S(2)}) collective-permute-start(bf16[4,6,256,256]{3,2,1,0:T(8,128)(2,1)} %all-gather.9.cloned.1.call-done.refs_0_), channel_id=1, source_target_pairs={{0,1},{1,0},{2,3},{3,2},{4,5},{5,4},{6,7},{7,6},{8,9},{9,8},{10,11... | collective-permute-start | bytes 9437192 | tf_op jit(solution)/shard_map/ppermute | solution.py:570
  576.1 5.8 collective-permute-start.11
  658.5 512.7 %reduce-scatter.5.cloned.1.call-start = ((), (), s32[]{:S(2)}) async-start(), calls=%async_computation.8 | async-start | bytes 13369344 | tf_op jit(solution)/shard_map/reduce_scatter | solution.py:655
  658.5 92.9 %collective-permute-start.13 = (bf16[4,6,256,256]{3,2,1,0:T(8,128)(2,1)}, bf16[4,6,256,256]{3,2,1,0:T(8,128)(2,1)S(1)}, u32[]{:S(2)}, u32[]{:S(2)}) collective-permute-start(bf16[4,6,256,256]{3,2,1,0:T(8,128)(2,1)} %all-gather.11.cloned.1.call-done.refs_0_), channel_id=1, source_target_pairs={{0,2},{1,3},{2,0},{3,1},{4,6},{5,7},{6,4},{7,5},{8,10},{9,11},{10,... | collective-permute-start | bytes 9437192 | tf_op jit(solution)/shard_map/ppermute | solution.py:569
  658.9 93.4 %collective-permute-start.12 = (bf16[4,6,256,256]{3,2,1,0:T(8,128)(2,1)}, bf16[4,6,256,256]{3,2,1,0:T(8,128)(2,1)}, u32[]{:S(2)}, u32[]{:S(2)}) collective-permute-start(bf16[4,6,256,256]{3,2,1,0:T(8,128)(2,1)} %all-gather.11.cloned.1.call-done.refs_0_), channel_id=1, source_target_pairs={{0,1},{1,0},{2,3},{3,2},{4,5},{5,4},{6,7},{7,6},{8,9},{9,8},{10,11... | collective-permute-start | bytes 9437192 | tf_op jit(solution)/shard_map/ppermute | solution.py:570
  751.4 5.8 collective-permute-start.14
  868.5 305.9 %collective-permute-start.16 = (f32[1536,1024]{1,0:T(8,128)}, f32[1536,1024]{1,0:T(8,128)}, u32[]{:S(2)}, u32[]{:S(2)}) collective-permute-start(f32[1536,1024]{1,0:T(8,128)} %get-tuple-element.95), channel_id=1, source_target_pairs={{0,4},{4,0},{1,5},{5,1},{2,6},{6,2},{3,7},{7,3},{8,12},{12,8},{9,1... | collective-permute-start | bytes 18874376 | tf_op jit(solution)/shard_map/ppermute | solution.py:663
  874.0 335.1 %collective-permute-start.15 = (f32[1536,1024]{1,0:T(8,128)}, f32[1536,1024]{1,0:T(8,128)}, u32[]{:S(2)}, u32[]{:S(2)}) collective-permute-start(f32[1536,1024]{1,0:T(8,128)} %get-tuple-element.93), channel_id=1, source_target_pairs={{0,4},{4,0},{1,5},{5,1},{2,6},{6,2},{3,7},{7,3},{8,12},{12,8},{9,1... | collective-permute-start | bytes 18874376 | tf_op jit(solution)/shard_map/ppermute | solution.py:662
  926.1 248.1 %collective-permute-start.19 = (bf16[3,6,256,256]{3,2,1,0:T(8,128)(2,1)}, bf16[3,6,256,256]{3,2,1,0:T(8,128)(2,1)}, u32[]{:S(2)}, u32[]{:S(2)}) collective-permute-start(bf16[3,6,256,256]{3,2,1,0:T(8,128)(2,1)} %pad_maximum_fusion.1.refs_0_), channel_id=1, source_target_pairs={{0,2},{1,3},{2,0},{3,1},{4,6},{5,7},{6,4},{7,5},{8,10},{9,11},{10,... | collective-permute-start | bytes 7077896 | tf_op jit(solution)/shard_map/ppermute | solution.py:569
  932.4 209.0 %collective-permute-start.17 = (f32[1536,16]{0,1:T(8,128)S(1)}, f32[1536,16]{0,1:T(8,128)S(1)}, u32[]{:S(2)}, u32[]{:S(2)}) collective-permute-start(f32[1536,16]{0,1:T(8,128)S(1)} %copy.108), channel_id=1, source_target_pairs={{0,4},{4,0},{1,5},{5,1},{2,6},{6,2},{3,7},{7,3},{8,12},{12,8},{9,1... | collective-permute-start | bytes 294920 | tf_op jit(solution)/shard_map/ppermute | solution.py:661
  1142.6 14.2 %copy-start.24 = (s32[1536]{0:T(1024)S(1)}, s32[1536]{0:T(1024)}, u32[]{:S(2)}) copy-start(s32[1536]{0:T(1024)} %copy-done.23) | copy-start | bytes 18436
  1168.6 52.0 %collective-permute-start.18 = (bf16[3,6,256,256]{3,2,1,0:T(8,128)(2,1)}, bf16[3,6,256,256]{3,2,1,0:T(8,128)(2,1)}, u32[]{:S(2)}, u32[]{:S(2)}) collective-permute-start(bf16[3,6,256,256]{3,2,1,0:T(8,128)(2,1)} %pad_maximum_fusion.1.refs_0_), channel_id=1, source_target_pairs={{0,1},{1,0},{2,3},{3,2},{4,5},{5,4},{6,7},{7,6},{8,9},{9,8},{10,11... | collective-permute-start | bytes 7077896 | tf_op jit(solution)/shard_map/ppermute | solution.py:570
  1171.1 37.6 %collective-permute-start.22 = (bf16[1,6,256,256]{3,2,1,0:T(8,128)(2,1)}, bf16[1,6,256,256]{3,2,1,0:T(8,128)(2,1)}, u32[]{:S(2)}, u32[]{:S(2)}) collective-permute-start(bf16[1,6,256,256]{3,2,1,0:T(8,128)(2,1)} %reduce-scatter.5.cloned.1.call-done), channel_id=1, source_target_pairs={{0,2},{1,3},{2,0},{3,1},{4,6},{5,7},{6,4},{7,5},{8,10},{9,11},{10,... | collective-permute-start | bytes 2359304 | tf_op jit(solution)/shard_map/ppermute | solution.py:569
  1174.2 46.4 %collective-permute-start.20 = (bf16[3,6,256,256]{3,2,1,0:T(8,128)(2,1)}, bf16[3,6,256,256]{3,2,1,0:T(8,128)(2,1)}, u32[]{:S(2)}, u32[]{:S(2)}) collective-permute-start(bf16[3,6,256,256]{3,2,1,0:T(8,128)(2,1)} %collective-permute-done.19.refs_2_), channel_id=1, source_target_pairs={{0,1},{1,0},{2,3},{3,2},{4,5},{5,4},{6,7},{7,6},{8,9},{9,8},{10,11... | collective-permute-start | bytes 7077896 | tf_op jit(solution)/shard_map/ppermute | solution.py:570
  1174.5 34.6 %copy-start.2 = (bf16[1536,1024]{1,0:T(8,128)(2,1)S(1)}, bf16[1536,1024]{1,0:T(8,128)(2,1)}, u32[]{:S(2)}) copy-start(bf16[1536,1024]{1,0:T(8,128)(2,1)} %dy_ref.1) | copy-start | bytes 9437188
  1174.5 34.6 %copy-start.45 = (f32[1536]{0:T(1024)S(1)}, f32[1536]{0:T(1024)}, u32[]{:S(2)}) copy-start(f32[1536]{0:T(1024)} %get-tuple-element.173) | copy-start | bytes 18436
  1208.6 12.0 collective-permute-start.21
  1208.7 11.9 collective-permute-start.23
  (31 other events, 264.9 us)
Sparse Core Ops, SparseCore 0:
  18.4 62.3 all-gather.4
  82.9 62.0 all-gather.6
  146.6 62.0 all-gather.8
  210.2 64.1 all-gather.10
  313.1 146.8 reduce-scatter.6
  484.0 143.6 reduce-scatter.8
  658.6 142.9 reduce-scatter.10
  814.7 139.8 reduce-scatter.4
where the time goes:
time: 1250 us; the launch traced here: 1240 us
  waiting for transfers between devices  563 us (45%)
  Pallas kernels  513 us (41%)
  local copies, waits for them, and re-layouts  65.7 us (5%)
  other arithmetic  46.3 us (4%)
  starting transfers between devices  22.8 us (2%)
  between operations  17 us (1%)
    pallas_call x4, Pallas kernels, run_experts(): pl.pallas_call(expert_kernel, out_shape=(jax.ShapeDtypeStruct((groups, ca...  287 us
    ppermute x6, waiting for transfers between devices, spread_slices(): other_x = lax.ppermute(own, 'b', to_x)  281 us
    ppermute x1, waiting for transfers between devices, block_of(): dk_back = lax.ppermute(total(dk_far), 'y', swap)  207 us
    pallas_call x2, Pallas kernels, combine(): pl.pallas_call(functools.partial(combine_kernel, experts, n_local), out_s...  94.4 us
    pallas_call x2, Pallas kernels, dispatch(): pl.pallas_call(functools.partial(dispatch_kernel, first, last, experts),...  89.6 us
    all_gather x4, waiting for transfers between devices, block_of(): gathered = lax.all_gather(offer[j], 'z')  52 us
    pallas_call x2, Pallas kernels, small_sum(): pl.pallas_call(body, out_shape=tuple((jax.ShapeDtypeStruct(v.shape, F32)...  32.8 us
  transfers between devices with their start and end apart: 32, of which 10 were waited for; matrix products, arithmetic and copies ran while one was open for 9% of the time, Pallas kernels for 41%

commit v1 on v0

v1 whole, which is shorter than its diff:
```python
import functools
import math
import jax
import jax.numpy as jnp
from jax import lax
from jax.experimental import pallas as pl
from jax.experimental.pallas import tpu as pltpu
from jax.sharding import Mesh, PartitionSpec as P


EPS = 1e-6
ALPHA = 0.001
AUX_SCALE = 0.25
BF = jnp.bfloat16
F32 = jnp.float32
CHUNK = 256
FAR_PARTS = 2
GROUP = 4
SEG = 128
ALIGN = 8
TILE = 256
LANES = 128
ANY = pl.BlockSpec(memory_space=pl.ANY)


def dot(a, b, dims=((1,), (0,))):
    return lax.dot_general(a, b, (dims, ((), ())), preferred_element_type=F32)


def offer_kernel(at_ref, gate, up, down, *refs):
    outs, (buf, sem_in, sem_out) = refs[:-3], refs[-3:]
    depth = buf.shape[-1]
    at = pl.ds(pl.multiple_of(at_ref[0] * depth, depth), depth)
    loads = []
    for j in range(len(outs)):
        mine = []
        for f in range(2):
            half = pl.ds(f * depth, depth)
            for t, src in enumerate((gate.at[j, at, half], up.at[j, at, half], down.at[j, half, at])):
                mine.append(pltpu.make_async_copy(src, buf.at[j, 2 * t + f], sem_in.at[j, 2 * t + f]))
        for cp in mine:
            cp.start()
        loads.append(mine)
    stores = []
    for j, mine in enumerate(loads):
        for cp in mine:
            cp.wait()
        stores.append(pltpu.make_async_copy(buf.at[j], outs[j], sem_out.at[j]))
        stores[-1].start()
    for cp in stores:
        cp.wait()


def offer(at, w_gate, w_up, w_down, depth):
    n_local = w_gate.shape[0]
    kinds = 3 * w_gate.shape[2] // depth
    return pl.pallas_call(
        offer_kernel,
        out_shape=tuple([jax.ShapeDtypeStruct((kinds, depth, depth), BF)] * n_local),
        grid_spec=pltpu.PrefetchScalarGridSpec(
            num_scalar_prefetch=1,
            grid=(),
            in_specs=[ANY] * 3,
            out_specs=[ANY] * n_local,
            scratch_shapes=[
                pltpu.VMEM((n_local, kinds, depth, depth), BF),
                pltpu.SemaphoreType.DMA((n_local, kinds)),
                pltpu.SemaphoreType.DMA((n_local,)),
            ],
        ),
        name="offer",
    )(at, w_gate, w_up, w_down)


def others_kernel(at_ref, src, out, buf, sem_in, sem_out):
    n = src.shape[0]
    loads = [
        pltpu.make_async_copy(src.at[lax.rem(at_ref[0] + 1 + q, n)], buf.at[q], sem_in.at[q]) for q in range(n - 1)
    ]
    stores = [pltpu.make_async_copy(buf.at[q], out.at[q], sem_out.at[q]) for q in range(n - 1)]
    for cp in loads:
        cp.start()
    for load, store in zip(loads, stores):
        load.wait()
        store.start()
    for cp in stores:
        cp.wait()


def others_of(at, gathered):
    n = gathered.shape[0]
    shape = (n - 1,) + gathered.shape[1:]
    return pl.pallas_call(
        others_kernel,
        out_shape=jax.ShapeDtypeStruct(shape, BF),
        grid_spec=pltpu.PrefetchScalarGridSpec(
            num_scalar_prefetch=1,
            grid=(),
            in_specs=[ANY],
            out_specs=ANY,
            scratch_shapes=[pltpu.VMEM(shape, BF), pltpu.SemaphoreType.DMA((n - 1,)), pltpu.SemaphoreType.DMA((n - 1,))],
        ),
        name="others",
    )(at, gathered)


def dispatch_kernel(first, last, experts, cnt, start, end, h_ref, dy_ref, rank_ref, w_ref, *refs):
    n_alias = 0 if first == 0 else 3
    hs, dys, wr, hbuf, dbuf, wbuf, hz, wz, hx, dx, wx, sem, xsem = refs[n_alias:]
    i = pl.program_id(0)
    c = i
    rows = lax.broadcasted_iota(jnp.int32, (SEG, CHUNK), 0)

    def copies(e, at):
        at = pl.multiple_of(at, ALIGN)
        return (
            pltpu.make_async_copy(hbuf.at[e], hs.at[e, pl.ds(at, SEG)], sem.at[0, e]),
            pltpu.make_async_copy(dbuf.at[e], dys.at[e, pl.ds(at, SEG)], sem.at[1, e]),
            pltpu.make_async_copy(wbuf.at[e], wr.at[e, pl.ds(at, SEG)], sem.at[2, e]),
        )

    def pick_of(e, base):
        same = rows + base == rank_ref[pl.ds(e, 1), :]
        weight = jnp.sum(jnp.where(same, w_ref[pl.ds(e, 1), :], 0.0), axis=1, keepdims=True)
        return jnp.where(same, 1.0, 0.0).astype(BF), jnp.broadcast_to(weight, (SEG, LANES))

    def group(q, carry):
        found = [pick_of(q * GROUP + u, 0) for u in range(GROUP)]
        pick = jnp.concatenate([v[0] for v in found], axis=0)
        for buf, src, what in ((hbuf, h_ref, 0), (dbuf, dy_ref, 1)):
            got = dot(pick, src[...]).astype(BF)

            @pl.when(i > 0)
            def _():
                for u in range(GROUP):
                    copies(q * GROUP + u, 0)[what].wait()

            for u in range(GROUP):
                e = q * GROUP + u
                buf[e] = got[u * SEG:(u + 1) * SEG]
                copies(e, start[c * experts + e])[what].start()

        @pl.when(i > 0)
        def _():
            for u in range(GROUP):
                copies(q * GROUP + u, 0)[2].wait()

        for u in range(GROUP):
            e = q * GROUP + u
            wbuf[e] = found[u][1]
            copies(e, start[c * experts + e])[2].start()
        return carry

    lax.fori_loop(0, experts // GROUP, group, 0)

    def overflow(e, carry):
        @pl.when(cnt[c * experts + e] > SEG)
        def _():
            pick, weight = pick_of(e, SEG)
            hx[...] = dot(pick, h_ref[...]).astype(BF)
            dx[...] = dot(pick, dy_ref[...]).astype(BF)
            wx[...] = weight
            at = pl.multiple_of(start[c * experts + e] + SEG, ALIGN)
            extra = (
                pltpu.make_async_copy(hx, hs.at[e, pl.ds(at, SEG)], xsem.at[0]),
                pltpu.make_async_copy(dx, dys.at[e, pl.ds(at, SEG)], xsem.at[1]),
                pltpu.make_async_copy(wx, wr.at[e, pl.ds(at, SEG)], xsem.at[2]),
            )
            for cp in extra:
                cp.start()
            for cp in extra:
                cp.wait()

        return carry

    lax.fori_loop(0, experts, overflow, 0)

    @pl.when(i == pl.num_programs(0) - 1)
    def _():
        def drain(e, carry):
            for cp in copies(e, 0):
                cp.wait()
            return carry

        lax.fori_loop(0, experts, drain, 0)
        if last:
            hz[...] = jnp.zeros_like(hz)
            wz[...] = jnp.zeros_like(wz)

            def fills(e):
                at = pl.multiple_of(end[e], ALIGN)
                return (
                    pltpu.make_async_copy(hz, hs.at[e, pl.ds(at, TILE)], sem.at[0, e]),
                    pltpu.make_async_copy(hz, dys.at[e, pl.ds(at, TILE)], sem.at[1, e]),
                    pltpu.make_async_copy(wz, wr.at[e, pl.ds(at, TILE)], sem.at[2, e]),
                )

            def fill(e, carry):
                for cp in fills(e):
                    cp.start()
                return carry

            def filled(e, carry):
                for cp in fills(e):
                    cp.wait()
                return carry

            lax.fori_loop(0, experts, fill, 0)
            lax.fori_loop(0, experts, filled, 0)


def dispatch(first, last, tables, h, dy, rank_t, w_t, cap, prev=None):
    tok, dim = h.shape
    experts = rank_t.shape[0]
    n = tok // CHUNK
    skip = max(first - 1, 0) * n
    shapes = (
        jax.ShapeDtypeStruct((experts, cap, dim), BF),
        jax.ShapeDtypeStruct((experts, cap, dim), BF),
        jax.ShapeDtypeStruct((experts, cap, LANES), F32),
    )
    prev = () if prev is None else prev
    return pl.pallas_call(
        functools.partial(dispatch_kernel, first, last, experts),
        out_shape=shapes,
        grid_spec=pltpu.PrefetchScalarGridSpec(
            num_scalar_prefetch=3,
            grid=(n,),
            in_specs=[
                pl.BlockSpec((CHUNK, dim), lambda i, *_: (i, 0)),
                pl.BlockSpec((CHUNK, dim), lambda i, *_: (i + skip, 0)),
                pl.BlockSpec((experts, CHUNK), lambda i, *_: (0, i)),
                pl.BlockSpec((experts, CHUNK), lambda i, *_: (0, i)),
            ] + [ANY] * len(prev),
            out_specs=[ANY] * 3,
            scratch_shapes=[
                pltpu.VMEM((experts, SEG, dim), BF),
                pltpu.VMEM((experts, SEG, dim), BF),
                pltpu.VMEM((experts, SEG, LANES), F32),
                pltpu.VMEM((TILE, dim), BF),
                pltpu.VMEM((TILE, LANES), F32),
                pltpu.VMEM((SEG, dim), BF),
                pltpu.VMEM((SEG, dim), BF),
                pltpu.VMEM((SEG, LANES), F32),
                pltpu.SemaphoreType.DMA((3, experts)),
                pltpu.SemaphoreType.DMA((3,)),
            ],
        ),
        input_output_aliases={7 + k: k for k in range(len(prev))},
        compiler_params=pltpu.CompilerParams(
            dimension_semantics=("arbitrary",), vmem_limit_bytes=40 << 20
        ),
        cost_estimate=pl.CostEstimate(
            flops=4 * n * experts * SEG * CHUNK * dim, bytes_accessed=n * experts * SEG * dim * 4, transcendentals=0
        ),
    )(*tables, h, dy, rank_t, w_t, *prev)


def expert_kernel(j, item_z, item_t, item_at, tiles, offs, total, h_ref, dy_ref, wr_ref, *refs):
    own, remote, (o_ref, dh_ref, dw_ref, gw_ref, acc_gu, acc_d, wbuf, sem) = refs[:3], refs[3:7], refs[7:]
    k = pl.program_id(0)
    i = item_t[k]
    turn = item_z[k]
    slot = lax.rem(turn, 2)
    live = k < total[0]
    block = wbuf.shape[-1]
    halves = range(2)
    parts = range(len(remote))

    def span(r):
        return pl.ds(pl.multiple_of(offs[r] * block, block), block)

    def own_copies():
        out = []
        for r in parts:
            for f in halves:
                half = pl.ds(f * block, block)
                for t, src in enumerate((own[0].at[j, span(r), half], own[1].at[j, span(r), half], own[2].at[j, half, span(r)])):
                    out.append(pltpu.make_async_copy(src, wbuf.at[0, r, 2 * t + f], sem.at[0, r, 2 * t + f]))
        return out

    def remote_copies(which):
        at = lax.rem(which, 2)
        return [pltpu.make_async_copy(remote[r].at[which - 1], wbuf.at[at, r], sem.at[at, r, 6]) for r in parts]

    @pl.when(k == 0)
    def _():
        for cp in own_copies():
            cp.start()
        for cp in own_copies():
            cp.wait()

    @pl.when(live & (i == 0) & (turn > 0))
    def _():
        for cp in remote_copies(turn):
            cp.wait()

    @pl.when(live & (i == 0) & (turn + 1 < tiles.shape[0]))
    def _():
        for cp in remote_copies(turn + 1):
            cp.start()

    @pl.when(live & (i == 0))
    def _():
        acc_gu[...] = jnp.zeros_like(acc_gu)
        acc_d[...] = jnp.zeros_like(acc_d)

    @pl.when(live)
    def _():
        h = [h_ref[0, :, span(r)] for r in parts]
        gate = [sum(dot(h[r], wbuf[slot, r, f]) for r in parts) for f in halves]
        up = [sum(dot(h[r], wbuf[slot, r, 2 + f]) for r in parts) for f in halves]
        sig = [jax.nn.sigmoid(v) for v in gate]
        act = [gate[f] * sig[f] for f in halves]
        hidden = [(act[f] * up[f]).astype(BF) for f in halves]
        for r in parts:
            o_ref[0, :, span(r)] = sum(dot(hidden[f], wbuf[slot, r, 4 + f]) for f in halves).astype(BF)
        dy_f = dy_ref[0].astype(F32)
        d_out = (dy_f * wr_ref[0][:, :1]).astype(BF)
        d_weight = jnp.sum(dy_f * o_ref[0].astype(F32), axis=1, keepdims=True)
        dw_ref[0] = jnp.broadcast_to(d_weight, dw_ref.shape[1:])
        g_ref = dh_ref
        g_ref[0] = d_out
        d_parts = [g_ref[0, :, span(r)] for r in parts]
        d_hidden = [sum(dot(d_parts[r], wbuf[slot, r, 4 + f], ((1,), (1,))) for r in parts) for f in halves]
        d_gate = [(d_hidden[f] * up[f] * sig[f] * (1.0 + gate[f] * (1.0 - sig[f]))).astype(BF) for f in halves]
        d_up = [(d_hidden[f] * act[f]).astype(BF) for f in halves]
        for f in halves:
            acc_d[f] += dot(hidden[f].T, d_out)
        h_t = h_ref[0].T
        for f in halves:
            acc_gu[f] += dot(h_t, d_gate[f])
            acc_gu[2 + f] += dot(h_t, d_up[f])
        for r in parts:
            dh_ref[0, :, span(r)] = sum(
                dot(d_gate[f], wbuf[slot, r, f], ((1,), (1,))) + dot(d_up[f], wbuf[slot, r, 2 + f], ((1,), (1,)))
                for f in halves
            ).astype(BF)

    @pl.when(live & (i == tiles[turn] - 1))
    def _():
        for r in parts:
            at = slice(r * block, (r + 1) * block)
            for f in range(4):
                gw_ref[0, r, f] = acc_gu[f, at, :].astype(BF)
            for f in halves:
                gw_ref[0, r, 4 + f] = acc_d[f, :, at].astype(BF)


def run_experts(j, n_local, steps, offs, hs, dys, wr, own, remote):
    _, cap, dim = hs.shape
    others, kinds, depth, _ = remote[0].shape
    groups = others + 1
    slices = len(remote)
    ff = kinds // 3 * depth

    def row_map(k, zs, ts, at, *_):
        return (at[k] * n_local + j, ts[k], 0)

    def out_map(k, zs, ts, at, *_):
        return (at[k], ts[k], 0)

    return pl.pallas_call(
        functools.partial(expert_kernel, j),
        out_shape=(
            jax.ShapeDtypeStruct((groups, cap, dim), BF),
            jax.ShapeDtypeStruct((groups, cap, dim), BF),
            jax.ShapeDtypeStruct((groups, cap, LANES), F32),
            jax.ShapeDtypeStruct((groups, slices, kinds, depth, depth), BF),
        ),
        grid_spec=pltpu.PrefetchScalarGridSpec(
            num_scalar_prefetch=6,
            grid=(steps[0].shape[0],),
            in_specs=[
                pl.BlockSpec((1, TILE, dim), row_map),
                pl.BlockSpec((1, TILE, dim), row_map),
                pl.BlockSpec((1, TILE, LANES), row_map),
            ] + [ANY] * (3 + slices),
            out_specs=[
                pl.BlockSpec((1, TILE, dim), out_map),
                pl.BlockSpec((1, TILE, dim), out_map),
                pl.BlockSpec((1, TILE, LANES), out_map),
                pl.BlockSpec((1, slices, kinds, depth, depth), lambda k, zs, ts, at, *_: (at[k], 0, 0, 0, 0)),
            ],
            scratch_shapes=[
                pltpu.VMEM((4, dim, depth), F32),
                pltpu.VMEM((2, depth, dim), F32),
                pltpu.VMEM((2, slices, kinds, depth, depth), BF),
                pltpu.SemaphoreType.DMA((2, slices, kinds + 1)),
            ],
        ),
        compiler_params=pltpu.CompilerParams(
            dimension_semantics=("arbitrary",), vmem_limit_bytes=56 << 20
        ),
        cost_estimate=pl.CostEstimate(
            flops=18 * groups * 4 * TILE * dim * ff, bytes_accessed=groups * 4 * TILE * dim * 8, transcendentals=0
        ),
    )(*steps[:4], offs, steps[4], hs, dys, wr, *own, *remote)


def combine_kernel(experts, n_local, cnt, start, limit, rank_ref, w_ref, *refs):
    outs, dhs, dws = refs[:n_local], refs[n_local:2 * n_local], refs[2 * n_local:3 * n_local]
    y_ref, dn_ref, dk_ref, obuf, dbuf, kbuf, sel, one, spread, ox, dx, kx, sem, xsem = refs[3 * n_local:]
    i = pl.program_id(0)
    n = pl.num_programs(0)
    slot = lax.rem(i, 2)
    lane = lax.broadcasted_iota(jnp.int32, (CHUNK, LANES), 1)
    row_lane = lax.broadcasted_iota(jnp.int32, (SEG, LANES), 1)

    def copies(step, s, e):
        z, j = divmod(e, n_local)
        at = pl.multiple_of(start[step * experts + e], ALIGN)
        return (
            pltpu.make_async_copy(outs[j].at[z, pl.ds(at, SEG)], obuf.at[s, pl.ds(e * SEG, SEG)], sem.at[s, 0, e]),
            pltpu.make_async_copy(dhs[j].at[z, pl.ds(at, SEG)], dbuf.at[s, pl.ds(e * SEG, SEG)], sem.at[s, 1, e]),
            pltpu.make_async_copy(dws[j].at[z, pl.ds(at, SEG)], kbuf.at[s, pl.ds(e * SEG, SEG)], sem.at[s, 2, e]),
        )

    @pl.when(i == 0)
    def _():
        for e in range(experts):
            for cp in copies(0, 0, e):
                cp.start()

    @pl.when(i + 1 < n)
    def _():
        for e in range(experts):
            for cp in copies(i + 1, 1 - slot, e):
                cp.start()

    def split(v):
        hi = v.astype(BF).astype(F32)
        mid = (v - hi).astype(BF).astype(F32)
        low = v - hi - mid
        return hi, mid, low

    rank = rank_ref[...]
    w_parts = split(w_ref[...])
    for e in range(experts):
        same = lane == rank[:, e:e + 1]
        at = slice(e * SEG, (e + 1) * SEG)
        one[:, at] = jnp.where(same, 1.0, 0.0).astype(BF)
        for p in range(3):
            sel[p * CHUNK:(p + 1) * CHUNK, at] = jnp.where(same, w_parts[p][:, e:e + 1], 0.0).astype(BF)

    for e in range(experts):
        for cp in copies(i, slot, e):
            cp.wait()

    def spread_of(e, value):
        parts = split(value)
        out = jnp.where(row_lane == e, parts[0], 0.0)
        out = jnp.where(row_lane == experts + e, parts[1], out)
        return jnp.where(row_lane == 2 * experts + e, parts[2], out).astype(BF)

    for e in range(experts):
        at = pl.ds(e * SEG, SEG)
        spread[at, :] = spread_of(e, kbuf[slot, at, :])
    three = dot(sel[...], obuf[slot])
    y_ref[...] = three[:CHUNK] + three[CHUNK:2 * CHUNK] + three[2 * CHUNK:]
    dn_ref[...] = dot(one[...], dbuf[slot])
    dk_ref[...] = dot(one[...], spread[...])

    for e in range(experts):
        z, j = divmod(e, n_local)

        @pl.when(cnt[i * experts + e] > SEG)
        def _():
            base = start[i * experts + e]
            at = pl.multiple_of(jnp.minimum(base + SEG, limit[e] - SEG), ALIGN)
            extra = (
                pltpu.make_async_copy(outs[j].at[z, pl.ds(at, SEG)], ox, xsem.at[0]),
                pltpu.make_async_copy(dhs[j].at[z, pl.ds(at, SEG)], dx, xsem.at[1]),
                pltpu.make_async_copy(dws[j].at[z, pl.ds(at, SEG)], kx, xsem.at[2]),
            )
            for cp in extra:
                cp.start()
            for cp in extra:
                cp.wait()
            seen = rank_ref[:, e:e + 1]
            same = (lane + (at - base) == seen) & (seen >= SEG)
            pick = jnp.where(same, 1.0, 0.0).astype(BF)
            parts = split(w_ref[:, e:e + 1])
            for p in range(3):
                y_ref[...] += dot(jnp.where(same, parts[p], 0.0).astype(BF), ox[...])
            dn_ref[...] += dot(pick, dx[...])
            dk_ref[...] += dot(pick, spread_of(e, kx[...]))


def combine(tables, rank, w, outs, dhs, dws):
    tok = rank.shape[0]
    n_local = len(outs)
    groups, _, dim = outs[0].shape
    experts = groups * n_local
    n = tok // CHUNK
    return pl.pallas_call(
        functools.partial(combine_kernel, experts, n_local),
        out_shape=(
            jax.ShapeDtypeStruct((tok, dim), F32),
            jax.ShapeDtypeStruct((tok, dim), F32),
            jax.ShapeDtypeStruct((tok, LANES), F32),
        ),
        grid_spec=pltpu.PrefetchScalarGridSpec(
            num_scalar_prefetch=3,
            grid=(n,),
            in_specs=[
                pl.BlockSpec((CHUNK, experts), lambda i, *_: (i, 0)),
                pl.BlockSpec((CHUNK, experts), lambda i, *_: (i, 0)),
            ] + [ANY] * (3 * n_local),
            out_specs=[
                pl.BlockSpec((CHUNK, dim), lambda i, *_: (i, 0)),
                pl.BlockSpec((CHUNK, dim), lambda i, *_: (i, 0)),
                pl.BlockSpec((CHUNK, LANES), lambda i, *_: (i, 0)),
            ],
            scratch_shapes=[
                pltpu.VMEM((2, experts * SEG, dim), BF),
                pltpu.VMEM((2, experts * SEG, dim), BF),
                pltpu.VMEM((2, experts * SEG, LANES), F32),
                pltpu.VMEM((3 * CHUNK, experts * SEG), BF),
                pltpu.VMEM((CHUNK, experts * SEG), BF),
                pltpu.VMEM((experts * SEG, LANES), BF),
                pltpu.VMEM((SEG, dim), BF),
                pltpu.VMEM((SEG, dim), BF),
                pltpu.VMEM((SEG, LANES), F32),
                pltpu.SemaphoreType.DMA((2, 3, experts)),
                pltpu.SemaphoreType.DMA((3,)),
            ],
        ),
        compiler_params=pltpu.CompilerParams(
            dimension_semantics=("arbitrary",), vmem_limit_bytes=56 << 20
        ),
        cost_estimate=pl.CostEstimate(
            flops=8 * n * CHUNK * experts * SEG * dim, bytes_accessed=n * experts * SEG * dim * 4, transcendentals=0
        ),
        name="combine",
    )(*tables, rank, w, *outs, *dhs, *dws)


def small_sum_kernel(axes, sizes, whole_ref, split_ref, whole_out, split_out, got_w, got_s, mine, send, recv):
    n = math.prod(sizes)
    share = split_ref.shape[0] // n if split_ref is not None else 0
    me = 0
    for axis, size in zip(axes, sizes):
        me = me * size + lax.axis_index(axis)

    def place(p):
        out = []
        for size in reversed(sizes):
            out.append(lax.rem(p, size))
            p = p // size
        return dict(zip(axes, reversed(out)))

    barrier = pltpu.get_barrier_semaphore()
    for k in range(1, n):
        pl.semaphore_signal(barrier, inc=1, device_id=place(lax.rem(me + k, n)), device_id_type=pl.DeviceIdType.MESH)
    pl.semaphore_wait(barrier, n - 1)

    def copy(src, dst, what, k):
        peer = lax.rem(me + k, n)
        return pltpu.make_async_remote_copy(
            src_ref=src, dst_ref=dst, send_sem=send.at[what, k], recv_sem=recv.at[what, k],
            device_id=place(peer), device_id_type=pl.DeviceIdType.MESH,
        )

    def rows_of(p):
        return split_ref.at[pl.ds(pl.multiple_of(p * share, 8), share)]

    first = []
    for k in range(1, n):
        first.append(copy(whole_ref, got_w.at[me], 0, k))
        if split_ref is not None:
            first.append(copy(rows_of(lax.rem(me + k, n)), got_s.at[me], 1, k))
    for cp in first:
        cp.start()
    got_w[me] = whole_ref[...]
    if split_ref is not None:
        got_s[me] = split_ref[pl.ds(pl.multiple_of(me * share, 8), share)]
    for cp in first:
        cp.wait()
    whole_out[...] = jnp.sum(got_w[...], axis=0)
    if split_ref is not None:
        mine[...] = jnp.sum(got_s[...], axis=0)
        own = pl.ds(pl.multiple_of(me * share, 8), share)
        split_out[own, :] = mine[...]
        second = [copy(mine, split_out.at[own], 2, k) for k in range(1, n)]
        for cp in second:
            cp.start()
        for cp in second:
            cp.wait()


def small_sum(axes, sizes, ident, whole, split=None):
    n = math.prod(sizes)
    vmem = pl.BlockSpec(memory_space=pltpu.VMEM)
    scratch = [pltpu.VMEM((n,) + whole.shape, F32)]
    if split is not None:
        scratch += [pltpu.VMEM((n, split.shape[0] // n, LANES), F32), pltpu.VMEM((split.shape[0] // n, LANES), F32)]
    scratch += [pltpu.SemaphoreType.DMA((3, n)), pltpu.SemaphoreType.DMA((3, n))]
    kernel = functools.partial(small_sum_kernel, axes, sizes)
    if split is None:
        def body(w, wo, gw, ss, rs):
            kernel(w, None, wo, None, gw, None, None, ss, rs)

        args = (whole,)
    else:
        body = kernel
        args = (whole, split)
    out = pl.pallas_call(
        body,
        out_shape=tuple(jax.ShapeDtypeStruct(v.shape, F32) for v in args),
        in_specs=[vmem] * len(args),
        out_specs=tuple([vmem] * len(args)),
        scratch_shapes=scratch,
        compiler_params=pltpu.CompilerParams(collective_id=ident, has_side_effects=True),
    )(*args)
    return out


def assemble_kernel(first, offs, *refs):
    pieces, refs = refs[:4], refs[4:]
    gate, up, down, buf, sem_in, sem_out = refs[-6:]
    slices, count, _, block, _ = buf.shape
    experts = pl.ds(first, count)
    loads = [pltpu.make_async_copy(pieces[r], buf.at[r], sem_in.at[r]) for r in range(slices)]
    for cp in loads:
        cp.start()
    stores = []
    for r in range(slices):
        loads[r].wait()
        at = pl.ds(pl.multiple_of(offs[r] * block, block), block)
        for f in range(2):
            part = pl.ds(f * block, block)
            for t, target in enumerate((gate.at[experts, at, part], up.at[experts, at, part], down.at[experts, part, at])):
                cp = pltpu.make_async_copy(buf.at[r, :, 2 * t + f], target, sem_out.at[r, 2 * t + f])
                cp.start()
                stores.append(cp)
    for cp in stores:
        cp.wait()


def assemble(first, offs, pieces, shapes, prev=()):
    count, kinds, depth = pieces[0].shape[:3]
    slices = len(pieces)
    return pl.pallas_call(
        functools.partial(assemble_kernel, first),
        out_shape=tuple(jax.ShapeDtypeStruct(v, BF) for v in shapes),
        grid_spec=pltpu.PrefetchScalarGridSpec(
            num_scalar_prefetch=1,
            grid=(),
            in_specs=[ANY] * (slices + len(prev)),
            out_specs=[ANY] * 3,
            scratch_shapes=[
                pltpu.VMEM((slices, count, kinds, depth, depth), BF),
                pltpu.SemaphoreType.DMA((slices,)),
                pltpu.SemaphoreType.DMA((slices, kinds)),
            ],
        ),
        input_output_aliases={1 + slices + k: k for k in range(len(prev))},
        compiler_params=pltpu.CompilerParams(vmem_limit_bytes=24 << 20),
    )(offs, *pieces, *prev)


def finish_kernel(x_ref, near_ref, back_ref, *refs):
    refs[-1][...] = (x_ref[...].astype(F32) + (near_ref[...] + back_ref[...])).astype(BF)


def finish(part, x, near, back, prev=()):
    tok, dim = x.shape
    n = back.shape[0] // CHUNK
    at = pl.BlockSpec((CHUNK, dim), lambda i: (i + part * n, 0))
    return pl.pallas_call(
        finish_kernel,
        out_shape=jax.ShapeDtypeStruct((tok, dim), BF),
        grid=(n,),
        in_specs=[at, at, pl.BlockSpec((CHUNK, dim), lambda i: (i, 0))] + [ANY] * len(prev),
        out_specs=at,
        input_output_aliases={3: 0} if prev else {},
        cost_estimate=pl.CostEstimate(flops=2 * back.size, bytes_accessed=12 * back.size, transcendentals=0),
    )(x, near, back, *prev)


def layout_tables(mask):
    tok, experts = mask.shape
    n = tok // CHUNK
    m3 = mask.reshape(n, CHUNK, experts)
    before = jnp.tril(jnp.ones((CHUNK, CHUNK), BF), -1)
    rank = jnp.einsum('ts,cse->cte', before, m3.astype(BF), preferred_element_type=F32)
    rank = jnp.where(m3 > 0, rank, -1.0).astype(jnp.int32).reshape(tok, experts)
    cnt = jnp.sum(m3, axis=1).astype(jnp.int32)
    return rank, cnt


def expert_steps(tiles, z_at, most):
    groups, n_local = tiles.shape
    turned = sum(jnp.where(z_at == q, jnp.roll(tiles, -q, axis=0), 0) for q in range(groups))
    ends = jnp.cumsum(turned, axis=0)
    steps = jnp.arange(groups * most, dtype=jnp.int32)[:, None]
    item_z = jnp.minimum(sum((steps >= ends[None, z]).astype(jnp.int32) for z in range(groups)), groups - 1)
    first = sum(jnp.where(item_z == z, (ends - turned)[None, z], 0) for z in range(groups))
    item_t = jnp.minimum(steps, ends[-1:] - 1) - first
    item_at = lax.rem(item_z + z_at, groups)
    return [(item_z[:, j], item_t[:, j], item_at[:, j], turned[:, j], ends[-1, j:j + 1]) for j in range(n_local)]


def windows(tables, rank, limit):
    experts = limit.shape[0]
    cnt, start = tables[0].reshape(-1, experts), tables[1].reshape(-1, experts)
    at = jnp.minimum(start, limit[None, :] - SEG)
    shift = start - at
    rank = rank.reshape(-1, CHUNK, experts)
    rank = jnp.where(rank >= 0, rank + shift[:, None, :], -1).reshape(-1, experts)
    return ((cnt + shift).reshape(-1), at.reshape(-1), limit), rank


def solution(mesh):
    ep_size = mesh.shape['ep']
    dp_size = mesh.shape['dp']
    n_dev = ep_size * dp_size
    nz, ny = ep_size // 2, 2
    fine = Mesh(mesh.devices.reshape(nz, ny, dp_size), ('z', 'y', 'b'))
    row_spec = P(('z', 'y', 'b'), None)
    exp_spec = P(('z', 'y'), None, None)
    swap = [(0, 1), (1, 0)]
    to_x = [(q, q ^ 2) for q in range(dp_size)]
    to_core = [(q, q ^ 1) for q in range(dp_size)]

    def spread_slices(own):
        other_x = send(own, 'b', to_x)
        return (own, send(own, 'b', to_core), other_x, send(other_x, 'b', to_core))

    def send(v, axis, pairs):
        return lax.ppermute(v, axis, pairs)

    def block_of(hidden_in, topk_idx, grad_out, norm_gain, w_router, w_gate, w_up, w_down):
        tok, dim = hidden_in.shape
        experts = w_router.shape[1]
        top_k = topk_idx.shape[1]
        n_local, _, _ = w_gate.shape
        tok_total = tok * n_dev
        mine = nz * n_local
        chunks = tok // CHUNK
        per_dev = tok * top_k // experts + tok * top_k // (2 * experts)
        cap = -(-(2 * per_dev + 2 * chunks * (ALIGN - 1)) // TILE) * TILE + TILE
        depth = dim // dp_size
        z_at = lax.axis_index('z')
        y_at = lax.axis_index('y')
        b_at = lax.axis_index('b')
        offs = jnp.bitwise_xor(b_at, jnp.arange(dp_size, dtype=jnp.int32))

        part = tok // FAR_PARTS
        dy_far = send(grad_out, 'y', swap)

        offers = offer(b_at.reshape(1), w_gate, w_up, w_down, depth)
        pieces = []
        for j in range(n_local):
            gathered = lax.all_gather(offers[j], 'z')
            pieces.append(spread_slices(others_of(z_at.reshape(1), gathered)))

        x_f = hidden_in.astype(F32)
        inv_rms = lax.rsqrt(jnp.mean(x_f * x_f, axis=-1, keepdims=True) + EPS)
        normed = (x_f * inv_rms * norm_gain).astype(BF)
        h_far = [send(normed[p * part:(p + 1) * part], 'y', swap) for p in range(FAR_PARTS)]
        logits = jnp.dot(normed, w_router, preferred_element_type=F32)
        probs = jax.nn.softmax(logits, axis=-1)
        eye = jnp.arange(experts, dtype=jnp.int32)
        mask = jnp.zeros((tok, experts), F32)
        for k in range(top_k):
            mask = mask + (topk_idx[:, k:k + 1] == eye[None, :]).astype(F32)
        chosen = mask * probs
        chosen_sum = jnp.sum(chosen, axis=1, keepdims=True)
        weights = chosen / chosen_sum

        def halves(v):
            v4 = v.reshape(tok, nz, ny, n_local)
            a, b = v4[:, :, 0].reshape(tok, mine), v4[:, :, 1].reshape(tok, mine)
            own = jnp.where(y_at == 0, a, b)
            return own, jnp.where(y_at == 0, b, a)

        m_near, m_send = halves(mask)
        w_near, w_send = halves(weights)
        stats_own = jnp.pad(jnp.stack([jnp.sum(mask, axis=0), jnp.sum(probs, axis=0)]), ((0, 6), (0, 0)))
        far = send(jnp.concatenate([jnp.concatenate([m_send, w_send], axis=1), stats_own], axis=0), 'y', swap)

        rank_near, cnt_near = layout_tables(m_near)
        pad_near = (cnt_near + ALIGN - 1) // ALIGN * ALIGN
        end_near = jnp.cumsum(pad_near, axis=0)
        near = (cnt_near.reshape(-1), (end_near - pad_near).reshape(-1), end_near[-1])

        rows = dispatch(0, False, near, normed, grad_out, rank_near.T, w_near.T, cap)

        far, marks = lax.optimization_barrier((far, rows[2]))
        rows = (rows[0], rows[1], marks)
        m_far, w_far, stats_far = far[:tok, :mine], far[:tok, mine:], far[tok:]
        rank_far, cnt_far = layout_tables(m_far)
        pad_far = (cnt_far + ALIGN - 1) // ALIGN * ALIGN
        end_far = jnp.cumsum(pad_far, axis=0) + end_near[-1]
        end = end_far[-1]
        far_t = (cnt_far.reshape(-1), (end_far - pad_far).reshape(-1), end)
        used = ((end + TILE - 1) // TILE).reshape(nz, n_local)
        limit = used.reshape(-1) * TILE
        steps = expert_steps(used, z_at, cap // TILE - 1)

        def window_parts(tables, rank, w, parts):
            (c, at, lim), rank = windows(tables, rank, limit)
            n, m = c.shape[0] // parts, tok // parts
            return [
                ((c[p * n:(p + 1) * n], at[p * n:(p + 1) * n], lim), rank[p * m:(p + 1) * m], w[p * m:(p + 1) * m])
                for p in range(parts)
            ]

        far_windows = window_parts(far_t, rank_far, w_far, FAR_PARTS)
        near_windows = window_parts(near, rank_near, w_near, 1)
        far_rank, far_w = rank_far.T, w_far.T
        far_t, far_rank, far_w, steps, far_windows, near_windows = lax.optimization_barrier(
            (far_t, far_rank, far_w, steps, far_windows, near_windows)
        )
        for p in range(FAR_PARTS):
            n = far_t[0].shape[0] // FAR_PARTS
            table = (far_t[0][p * n:(p + 1) * n], far_t[1][p * n:(p + 1) * n], far_t[2])
            at_p = slice(p * part, (p + 1) * part)
            rows = dispatch(
                1 + p, p == FAR_PARTS - 1, table, h_far[p], dy_far, far_rank[:, at_p], far_w[:, at_p], cap, rows
            )

        outs, dhs, dws, sums = [], [], [], []
        for j in range(n_local):
            o, dh, dw, gw = run_experts(j, n_local, steps[j], offs, *rows, (w_gate, w_up, w_down), pieces[j])
            steps, dw = lax.optimization_barrier((steps, dw))
            outs.append(o)
            dhs.append(dh)
            dws.append(dw)
            if j < n_local - 1:
                sums.append(lax.psum_scatter(gw.reshape((nz * dp_size,) + gw.shape[2:]), ('z', 'b'), scatter_dimension=0))

        def total(v):
            return v[:, :mine] + v[:, mine:2 * mine] + v[:, 2 * mine:3 * mine]

        returned, ties = [], []
        for args in far_windows:
            y_far, dn_far, dk_far = combine(*args, outs, dhs, dws)
            ties.append(dk_far)
            returned.append((send(total(dk_far), 'y', swap), send(dn_far, 'y', swap), send(y_far, 'y', swap)))
        stats_in = jnp.pad(stats_own + stats_far, ((0, 0), (0, LANES - experts)))
        gw, stats_in, *_ = lax.optimization_barrier((gw, stats_in, *ties))
        (stats,) = small_sum(('z', 'b'), (nz, dp_size), 0, stats_in)
        gw, stats = lax.optimization_barrier((gw, stats))
        slice_of = [lax.dynamic_index_in_dim(gw, offs[r], 1, keepdims=False) for r in range(dp_size)]
        core_own = send(slice_of[1], 'b', to_core)
        core_x = send(slice_of[3], 'b', to_core)
        for_x = (slice_of[2].astype(F32) + core_x.astype(F32)).astype(BF)
        from_x = send(for_x, 'b', to_x)
        mine_sum = slice_of[0].astype(F32) + core_own.astype(F32) + from_x.astype(F32)
        sums.append(lax.psum_scatter(mine_sum.astype(BF), 'z', scatter_dimension=0))
        dk_back, dn_back = (jnp.concatenate([v[q] for v in returned], axis=0) for q in range(2))
        y_back = [v[2] for v in returned]
        y_near, dn_near, dk_near = combine(*near_windows[0], outs, dhs, dws)

        load_frac = stats[0, :experts] / (top_k * tok_total)
        aux_loss = ALPHA * experts * jnp.sum(load_frac * stats[1, :experts] / tok_total)
        near4 = total(dk_near).reshape(tok, nz, n_local)
        back4 = dk_back.reshape(tok, nz, n_local)
        d_weight = jnp.stack([jnp.where(y_at == 0, near4, back4), jnp.where(y_at == 0, back4, near4)], axis=2).reshape(tok, experts)
        d_chosen = (d_weight - jnp.sum(weights * d_weight, axis=1, keepdims=True)) / chosen_sum
        aux_coef = AUX_SCALE * math.sqrt(dim * experts) * experts
        d_prob = mask * d_chosen + aux_coef * load_frac[None, :]
        d_logit = probs * (d_prob - jnp.sum(probs * d_prob, axis=1, keepdims=True))
        d_logit_bf = d_logit.astype(BF)
        router_part = jnp.einsum('td,te->de', normed, d_logit_bf, preferred_element_type=F32)
        d_normed = dn_near + dn_back + jnp.einsum('te,de->td', d_logit_bf, w_router, preferred_element_type=F32)
        gain_part = jnp.sum(d_normed * x_f * inv_rms, axis=0)
        d_scaled = d_normed * norm_gain
        inv_cube = inv_rms * inv_rms * inv_rms
        grad_in = (grad_out.astype(F32) + inv_rms * d_scaled - x_f * inv_cube * jnp.mean(d_scaled * x_f, axis=-1, keepdims=True)).astype(BF)
        sums_yz = small_sum(('z', 'b'), (nz, dp_size), 1, gain_part.reshape(-1, LANES), router_part.reshape(-1, LANES))
        both = jnp.concatenate(sums_yz, axis=0)
        both = both + send(both, 'y', swap)
        gain_rows = dim // LANES

        *early, grad_in, _ = lax.optimization_barrier((*sums[:-1], grad_in, sums_yz[0]))
        late, grad_in = lax.optimization_barrier((sums[-1], grad_in))
        shapes = (w_gate.shape, w_up.shape, w_down.shape)
        grads = assemble(0, offs, spread_slices(jnp.stack(early)), shapes)
        grads = assemble(n_local - 1, offs, spread_slices(late[None]), shapes, grads)
        block_out = ()
        for p in range(FAR_PARTS):
            block_out = (finish(p, hidden_in, y_near, y_back[p], block_out),)
        block_out = block_out[0]
        return (block_out, grad_in, aux_loss, both[:gain_rows].reshape(dim), both[gain_rows:].reshape(dim, experts), *grads)


    return jax.shard_map(
        block_of,
        mesh=fine,
        in_specs=(row_spec, row_spec, row_spec, P(None), P(None, None), exp_spec, exp_spec, exp_spec),
        out_specs=(row_spec, row_spec, P(), P(None), P(None, None), exp_spec, exp_spec, exp_spec),
        check_vma=False,
    )
```

time: 1250 us -> 1110 us (0.89)
  waiting for transfers between devices: 563 us -> 434 us
  Pallas kernels: 513 us -> 484 us
    ppermute x24 -> x32, waiting for transfers between devices: 511 us -> 433 us  [send(): return lax.ppermute(v, axis, pairs)]
    all_gather x4, waiting for transfers between devices: 52 us -> 0.04 us  [block_of(): gathered = lax.all_gather(offers[j], 'z')]
    pallas_call x5 -> x13, Pallas kernels: 297 us -> 276 us  [the longest x4 242 us: run_experts(): pl.pallas_call(functools.partial(expert_kernel, j), out_shape=(jax.ShapeD...]
    pallas_call x2 -> x3, Pallas kernels: 89.6 us -> 70.6 us  [dispatch(): pl.pallas_call(functools.partial(dispatch_kernel, first, last, experts),...]
    convert_element_type x0 -> x2, other arithmetic: none -> 12.8 us  [the longest x1 7.12 us: block_of(): sums.append(lax.psum_scatter(mine_sum.astype(BF), 'z', scatter_dimension=0))]
    pallas_call x2 -> x3, Pallas kernels: 94.4 us -> 99.1 us  [combine(): pl.pallas_call(functools.partial(combine_kernel, experts, n_local), out_s...]
  transfers between devices with their start and end apart: 32 -> 40, of which waited for: 10 -> 12; matrix products, arithmetic and copies ran while one was open for 9% -> 12% of each run, Pallas kernels for 41% -> 43%
where the time goes in v1:
time: 1110 us; the launch traced here: 1100 us
  Pallas kernels  484 us (44%)
  waiting for transfers between devices  434 us (39%)
  local copies, waits for them, and re-layouts  68.6 us (6%)
  other arithmetic  57.4 us (5%)
  between operations  24.9 us (2%)
  starting transfers between devices  19.1 us (2%)
    ppermute x32, waiting for transfers between devices, send(): return lax.ppermute(v, axis, pairs)  433 us
    pallas_call x4, Pallas kernels, run_experts(): pl.pallas_call(functools.partial(expert_kernel, j), out_shape=(jax.ShapeD...  242 us
    pallas_call x3, Pallas kernels, combine(): pl.pallas_call(functools.partial(combine_kernel, experts, n_local), out_s...  99.1 us
    pallas_call x3, Pallas kernels, dispatch(): pl.pallas_call(functools.partial(dispatch_kernel, first, last, experts),...  70.6 us
    pallas_call x2, Pallas kernels, small_sum(): pl.pallas_call(body, out_shape=tuple((jax.ShapeDtypeStruct(v.shape, F32)...  37.7 us
  transfers between devices with their start and end apart: 40, of which 12 were waited for; matrix products, arithmetic and copies ran while one was open for 12% of the time, Pallas kernels for 43%

profile of v1, /device:TPU:14, one launch (start us, length us, event | category | flops | bytes accessed | tf_op | source)
XLA Modules:
  0.0 1096.5 jit_solution(6556157764375474274)
XLA Ops:
  7.2 3.3 offer.1
  27.1 2.0 fusion.61
  39.4 30.4 %shard_map.143 = (bf16[16,1536,1024]{2,1,0:T(8,128)(2,1)}, bf16[16,1536,1024]{2,1,0:T(8,128)(2,1)}, f32[16,1536,128]{2,1,0:T(8,128)}) custom-call(s32[96]{0:T(128)S(1)} %convert_element_type.163.cnt, s32[96]{0:T(128)S(1)} %multiply_subtract_fusion.1.start, s32[16]{0:T(128)S(1)} %slice_reduce_fusion.end, bf16[1536,1024]{1,0:T(8,128)(2,1)S(1)} %fusion.2.h_ref, ...), custom_call_target="tpu_custom_call" | custom-call | flops 12884901888 | bytes 50331648 | tf_op jit(solution)/shard_map/pallas_call | solution.py:223
  78.8 2.6 others.4.refs_3_
  83.4 2.2 copy.157
  99.0 2.3 fusion.62
  102.5 31.2 %collective-permute-done.5.refs_5_ = bf16[3,6,256,256]{3,2,1,0:T(8,128)(2,1)} collective-permute-done((bf16[3,6,256,256]{3,2,1,0:T(8,128)(2,1)}, bf16[3,6,256,256]{3,2,1,0:T(8,128)(2,1)}, u32[]{:S(2)}, u32[]{:S(2)}) %collective-permute-start.5) | collective-permute-done | bytes 2359328 | tf_op jit(solution)/shard_map/ppermute | solution.py:732
  148.8 19.9 %collective-permute-done.2.dy_ref = bf16[1536,1024]{1,0:T(8,128)(2,1)} collective-permute-done((bf16[1536,1024]{1,0:T(8,128)(2,1)}, bf16[1536,1024]{1,0:T(8,128)(2,1)}, u32[]{:S(2)}, u32[]{:S(2)}) %collective-permute-start.2) | collective-permute-done | bytes 3145760 | tf_op jit(solution)/shard_map/ppermute | solution.py:732
  168.7 16.8 %shard_map.144 = (bf16[16,1536,1024]{2,1,0:T(8,128)(2,1)}, bf16[16,1536,1024]{2,1,0:T(8,128)(2,1)}, f32[16,1536,128]{2,1,0:T(8,128)}) custom-call(s32[48]{0:T(128)S(1)} %get-tuple-element.408.cnt, s32[48]{0:T(128)S(1)} %get-tuple-element.406.start, s32[16]{0:T(128)S(1)} %get-tuple-element.154.end, ...), custom_call_target="tpu_custom_call", output_to_operand_aliasing={{0}: (7, {}), {1}: (8, {}), {2}: (9, {})} | custom-call | flops 6442450944 | bytes 25165824 | tf_op jit(solution)/shard_map/pallas_call | solution.py:223
  185.6 23.3 %shard_map.145 = (bf16[16,1536,1024]{2,1,0:T(8,128)(2,1)}, bf16[16,1536,1024]{2,1,0:T(8,128)(2,1)}, f32[16,1536,128]{2,1,0:T(8,128)}) custom-call(s32[48]{0:T(128)S(1)} %get-tuple-element.409.cnt, s32[48]{0:T(128)S(1)} %get-tuple-element.407.start, s32[16]{0:T(128)S(1)} %get-tuple-element.154.end, ...), custom_call_target="tpu_custom_call", output_to_operand_aliasing={{0}: (7, {}), {1}: (8, {}), {2}: (9, {})} | custom-call | flops 6442450944 | bytes 25165824 | tf_op jit(solution)/shard_map/pallas_call | solution.py:223
  209.0 66.0 %shard_map.146 = (bf16[4,1536,1024]{2,1,0:T(8,128)(2,1)}, bf16[4,1536,1024]{2,1,0:T(8,128)(2,1)}, f32[4,1536,128]{2,1,0:T(8,128)}, bf16[4,4,6,256,256]{4,3,2,1,0:T(8,128)(2,1)}) custom-call(s32[20]{0:T(128)} %get-tuple-element.147.item_z, s32[20]{0:T(128)} %get-tuple-element.148.item_t, s32[20]{0:T(128)} %get-tuple-element.149.item_at, ...), custom_call_target="tpu_custom_call" | custom-call | flops 38654705664 | bytes 33554432 | tf_op jit(solution)/shard_map/pallas_call | solution.py:363
  275.4 2.6 others.5.refs_3_
  278.2 66.2 %collective-permute-done.8.refs_5_ = bf16[3,6,256,256]{3,2,1,0:T(8,128)(2,1)S(1)} collective-permute-done((bf16[3,6,256,256]{3,2,1,0:T(8,128)(2,1)}, bf16[3,6,256,256]{3,2,1,0:T(8,128)(2,1)S(1)}, u32[]{:S(2)}, u32[]{:S(2)}) %collective-permute-start.8) | collective-permute-done | bytes 2359328 | tf_op jit(solution)/shard_map/ppermute | solution.py:732
  344.4 4.6 collective-permute-done.9.refs_6_
  349.0 65.6 %shard_map.147 = (bf16[4,1536,1024]{2,1,0:T(8,128)(2,1)}, bf16[4,1536,1024]{2,1,0:T(8,128)(2,1)}, f32[4,1536,128]{2,1,0:T(8,128)}, bf16[4,4,6,256,256]{4,3,2,1,0:T(8,128)(2,1)}) custom-call(s32[20]{0:T(128)} %get-tuple-element.184.item_z, s32[20]{0:T(128)} %get-tuple-element.185.item_t, s32[20]{0:T(128)} %get-tuple-element.186.item_at, ...), custom_call_target="tpu_custom_call" | custom-call | flops 38654705664 | bytes 33554432 | tf_op jit(solution)/shard_map/pallas_call | solution.py:363
  414.7 2.6 others.6.refs_3_
  417.5 66.9 %collective-permute-done.11.refs_5_ = bf16[3,6,256,256]{3,2,1,0:T(8,128)(2,1)} collective-permute-done((bf16[3,6,256,256]{3,2,1,0:T(8,128)(2,1)}, bf16[3,6,256,256]{3,2,1,0:T(8,128)(2,1)}, u32[]{:S(2)}, u32[]{:S(2)}) %collective-permute-start.11) | collective-permute-done | bytes 2359328 | tf_op jit(solution)/shard_map/ppermute | solution.py:732
  484.4 2.6 others.7.refs_3_
  487.1 2.2 collective-permute-done.12.refs_6_
  489.3 62.7 %shard_map.148 = (bf16[4,1536,1024]{2,1,0:T(8,128)(2,1)}, bf16[4,1536,1024]{2,1,0:T(8,128)(2,1)}, f32[4,1536,128]{2,1,0:T(8,128)}, bf16[4,4,6,256,256]{4,3,2,1,0:T(8,128)(2,1)}) custom-call(s32[20]{0:T(128)} %get-tuple-element.202.item_z, s32[20]{0:T(128)} %get-tuple-element.203.item_t, s32[20]{0:T(128)} %get-tuple-element.204.item_at, ...), custom_call_target="tpu_custom_call" | custom-call | flops 38654705664 | bytes 33554432 | tf_op jit(solution)/shard_map/pallas_call | solution.py:363
  552.1 3.3 collective-permute-start.13
  555.4 10.9 collective-permute-done.14.refs_5_
  572.2 47.4 %shard_map.149 = (bf16[4,1536,1024]{2,1,0:T(8,128)(2,1)}, bf16[4,1536,1024]{2,1,0:T(8,128)(2,1)}, f32[4,1536,128]{2,1,0:T(8,128)}, bf16[4,4,6,256,256]{4,3,2,1,0:T(8,128)(2,1)}) custom-call(s32[20]{0:T(128)} %get-tuple-element.215.item_z, s32[20]{0:T(128)} %get-tuple-element.216.item_t, s32[20]{0:T(128)} %get-tuple-element.217.item_at, ...), custom_call_target="tpu_custom_call" | custom-call | flops 38654705664 | bytes 33554432 | tf_op jit(solution)/shard_map/pallas_call | solution.py:363
  619.5 26.1 %combine.5 = (f32[768,1024]{1,0:T(8,128)}, f32[768,1024]{1,0:T(8,128)}, f32[768,128]{1,0:T(8,128)}) custom-call(s32[48]{0:T(128)} %slice.353.cnt, s32[48]{0:T(128)} %slice.355.start, s32[16]{0:T(128)} %get-tuple-element.240.limit, s32[768,16]{1,0:T(8,128)} %bitcast.174, f32[768,16]{1,0:T(8,128)} %get-tuple-element.242.w_ref, ...), custom_call_target="tpu_custom_call" | custom-call | flops 12884901888 | bytes 25165824 | tf_op jit(solution)/shard_map/combine/pallas_call | solution.py:496
  645.7 26.6 %combine.4 = (f32[768,1024]{1,0:T(8,128)}, f32[768,1024]{1,0:T(8,128)}, f32[768,128]{1,0:T(8,128)}) custom-call(s32[48]{0:T(128)} %slice.360.cnt, s32[48]{0:T(128)} %slice.362.start, s32[16]{0:T(128)} %get-tuple-element.240.limit, s32[768,16]{1,0:T(8,128)} %bitcast.173, f32[768,16]{1,0:T(8,128)} %get-tuple-element.236.w_ref, ...), custom_call_target="tpu_custom_call" | custom-call | flops 12884901888 | bytes 25165824 | tf_op jit(solution)/shard_map/combine/pallas_call | solution.py:496
  672.3 13.0 %shard_map.152 = f32[8,128]{1,0:T(8,128)} custom-call(f32[8,128]{1,0:T(8,128)} %pad.9.w), custom_call_target="tpu_custom_call" | custom-call | tf_op jit(solution)/shard_map/pallas_call | solution.py:608
  685.3 6.2 dynamic-slice_bitcast_fusion.1
  698.2 2.0 collective-permute-start.21
  700.3 5.6 fusion.10
  707.4 46.4 %combine.3 = (f32[1536,1024]{1,0:T(8,128)}, f32[1536,1024]{1,0:T(8,128)}, f32[1536,128]{1,0:T(8,128)}) custom-call(s32[96]{0:T(128)} %get-tuple-element.142.cnt, s32[96]{0:T(128)} %get-tuple-element.143.start, s32[16]{0:T(128)} %get-tuple-element.240.limit, s32[1536,16]{1,0:T(8,128)} %bitcast.168, f32[1536,16]{1,0:T(8,128)} %copy.165.w_ref, ...), custom_call_target="tpu_custom_call" | custom-call | flops 25769803776 | bytes 50331648 | tf_op jit(solution)/shard_map/combine/pallas_call | solution.py:496
  757.4 95.5 %collective-permute-done.24 = f32[768,16]{1,0:T(8,128)S(1)} collective-permute-done((f32[768,16]{1,0:T(8,128)S(1)}, f32[768,16]{1,0:T(8,128)S(1)}, u32[]{:S(2)}, u32[]{:S(2)}) %collective-permute-start.24) | collective-permute-done | bytes 49184 | tf_op jit(solution)/shard_map/ppermute | solution.py:732
  854.7 2.0 copy.169
  858.2 2.0 copy.170
  866.4 7.1 fusion.12
  874.7 2.9 fusion.58
  877.7 2.0 reshape.373.split_ref
  879.7 2.1 fusion.59
  881.8 8.4 fusion.8
  890.2 24.7 %shard_map.153 = (f32[8,128]{1,0:T(8,128)}, f32[256,128]{1,0:T(8,128)}) custom-call(f32[8,128]{1,0:T(8,128)} %bitcast.179, f32[256,128]{1,0:T(8,128)} %reshape.373.split_ref), custom_call_target="tpu_custom_call" | custom-call | tf_op jit(solution)/shard_map/pallas_call | solution.py:608
  914.9 5.9 fusion.5
  925.6 51.1 %collective-permute-done.30.refs_2_ = bf16[3,6,256,256]{3,2,1,0:T(8,128)(2,1)} collective-permute-done((bf16[3,6,256,256]{3,2,1,0:T(8,128)(2,1)S(1)}, bf16[3,6,256,256]{3,2,1,0:T(8,128)(2,1)}, u32[]{:S(2)}, u32[]{:S(2)}) %collective-permute-start.30) | collective-permute-done | bytes 2359328 | tf_op jit(solution)/shard_map/ppermute | solution.py:732
  977.1 17.8 %collective-permute-done.17.back_ref = f32[768,1024]{1,0:T(8,128)} collective-permute-done((f32[768,1024]{1,0:T(8,128)}, f32[768,1024]{1,0:T(8,128)}, u32[]{:S(2)}, u32[]{:S(2)}) %collective-permute-start.17) | collective-permute-done | bytes 3145760 | tf_op jit(solution)/shard_map/ppermute | solution.py:732
  994.9 2.0 collective-permute-done.27.refs_2_
  996.9 64.4 %collective-permute-done.16.back_ref = f32[768,1024]{1,0:T(8,128)} collective-permute-done((f32[768,1024]{1,0:T(8,128)}, f32[768,1024]{1,0:T(8,128)}, u32[]{:S(2)}, u32[]{:S(2)}) %collective-permute-start.16) | collective-permute-done | bytes 3145760 | tf_op jit(solution)/shard_map/ppermute | solution.py:732
  1062.9 5.0 shard_map.150.refs_0_
  1067.9 5.0 shard_map.151
  1077.3 7.3 shard_map.154
  1084.6 3.6 shard_map.155
  (300 shorter events, 99.3 us)
Async XLA Ops:
  7.2 71.6 %all-gather.9.cloned.1.call-start = ((), (), s32[]{:S(2)}) async-start(), calls=%async_computation.8 | async-start | bytes 3932160 | tf_op jit(solution)/shard_map/all_gather | solution.py:756
  10.6 264.9 %all-gather.11.cloned.1.call-start = ((), (), s32[]{:S(2)}) async-start(), calls=%async_computation.9 | async-start | bytes 3932160 | tf_op jit(solution)/shard_map/all_gather | solution.py:756
  11.3 403.4 %all-gather.13.cloned.1.call-start = ((), (), s32[]{:S(2)}) async-start(), calls=%async_computation.10 | async-start | bytes 3932160 | tf_op jit(solution)/shard_map/all_gather | solution.py:756
  12.0 472.4 %all-gather.15.cloned.1.call-start = ((), (), s32[]{:S(2)}) async-start(), calls=%async_computation.11 | async-start | bytes 3932160 | tf_op jit(solution)/shard_map/all_gather | solution.py:756
  26.6 43.8 %collective-permute-start = (f32[1544,32]{0,1:T(8,128)}, f32[1544,32]{0,1:T(8,128)}, u32[]{:S(2)}, u32[]{:S(2)}) collective-permute-start(f32[1544,32]{0,1:T(8,128)} %pad_maximum_fusion.1), channel_id=1, source_target_pairs={{0,4},{4,0},{1,5},{5,1},{2,6},{6,2},{3,7},{7,3},{8,12},{12,8},{9,1... | collective-permute-start | bytes 592904 | tf_op jit(solution)/shard_map/ppermute | solution.py:732
  29.2 119.6 %collective-permute-start.3 = (bf16[768,1024]{1,0:T(8,128)(2,1)}, bf16[768,1024]{1,0:T(8,128)(2,1)}, u32[]{:S(2)}, u32[]{:S(2)}) collective-permute-start(bf16[768,1024]{1,0:T(8,128)(2,1)} %get-tuple-element.341), channel_id=1, source_target_pairs={{0,4},{4,0},{1,5},{5,1},{2,6},{6,2},{3,7},{7,3},{8,12},{12,8},{9,1... | collective-permute-start | bytes 4718600 | tf_op jit(solution)/shard_map/ppermute | solution.py:732
  30.8 154.8 %collective-permute-start.1 = (bf16[768,1024]{1,0:T(8,128)(2,1)}, bf16[768,1024]{1,0:T(8,128)(2,1)}, u32[]{:S(2)}, u32[]{:S(2)}) collective-permute-start(bf16[768,1024]{1,0:T(8,128)(2,1)} %get-tuple-element.342), channel_id=1, source_target_pairs={{0,4},{4,0},{1,5},{5,1},{2,6},{6,2},{3,7},{7,3},{8,12},{12,8},{9,1... | collective-permute-start | bytes 4718600 | tf_op jit(solution)/shard_map/ppermute | solution.py:732
  31.3 137.5 %collective-permute-start.2 = (bf16[1536,1024]{1,0:T(8,128)(2,1)}, bf16[1536,1024]{1,0:T(8,128)(2,1)}, u32[]{:S(2)}, u32[]{:S(2)}) collective-permute-start(bf16[1536,1024]{1,0:T(8,128)(2,1)} %dy_ref.1), channel_id=1, source_target_pairs={{0,4},{4,0},{1,5},{5,1},{2,6},{6,2},{3,7},{7,3},{8,12},{12,8},{9,1... | collective-permute-start | bytes 9437192 | tf_op jit(solution)/shard_map/ppermute | solution.py:732
  32.8 888.1 %reduce-scatter.7.cloned.1.call-start = ((), (), s32[]{:S(2)}) async-start(), calls=%async_computation.5 | async-start | bytes 13369344 | tf_op jit(solution)/shard_map/reduce_scatter | solution.py:833
  73.6 22.4 %copy-start.29 = (f32[1536,16]{0,1:T(8,128)S(1)}, f32[1536,16]{0,1:T(8,128)}, u32[]{:S(2)}) copy-start(f32[1536,16]{0,1:T(8,128)} %get-tuple-element.348) | copy-start | bytes 294916
  76.1 25.2 %copy-start.40 = (s32[4,4]{1,0:T(4,128)}, s32[4,4]{1,0:T(4,128)S(1)}, u32[]{:S(2)}) copy-start(s32[4,4]{1,0:T(4,128)S(1)} %fusion.51) | copy-start | bytes 196
  76.1 25.1 %copy-start.46 = (s32[4,4]{1,0:T(4,128)}, s32[4,4]{1,0:T(4,128)S(1)}, u32[]{:S(2)}) copy-start(s32[4,4]{1,0:T(4,128)S(1)} %reduce_window_sum.33) | copy-start | bytes 196
  81.4 52.2 %collective-permute-start.5 = (bf16[3,6,256,256]{3,2,1,0:T(8,128)(2,1)}, bf16[3,6,256,256]{3,2,1,0:T(8,128)(2,1)}, u32[]{:S(2)}, u32[]{:S(2)}) collective-permute-start(bf16[3,6,256,256]{3,2,1,0:T(8,128)(2,1)} %others.4.refs_3_), channel_id=1, source_target_pairs={{0,2},{1,3},{2,0},{3,1},{4,6},{5,7},{6,4},{7,5},{8,10},{9,11},{10,... | collective-permute-start | bytes 7077896 | tf_op jit(solution)/shard_map/ppermute | solution.py:732
  102.4 106.5 %collective-permute-start.4 = (bf16[3,6,256,256]{3,2,1,0:T(8,128)(2,1)}, bf16[3,6,256,256]{3,2,1,0:T(8,128)(2,1)}, u32[]{:S(2)}, u32[]{:S(2)}) collective-permute-start(bf16[3,6,256,256]{3,2,1,0:T(8,128)(2,1)} %others.4.refs_3_), channel_id=1, source_target_pairs={{0,1},{1,0},{2,3},{3,2},{4,5},{5,4},{6,7},{7,6},{8,9},{9,8},{10,11... | collective-permute-start | bytes 7077896 | tf_op jit(solution)/shard_map/ppermute | solution.py:732
  133.6 75.3 %collective-permute-start.6 = (bf16[3,6,256,256]{3,2,1,0:T(8,128)(2,1)}, bf16[3,6,256,256]{3,2,1,0:T(8,128)(2,1)}, u32[]{:S(2)}, u32[]{:S(2)}) collective-permute-start(bf16[3,6,256,256]{3,2,1,0:T(8,128)(2,1)} %collective-permute-done.5.refs_5_), channel_id=1, source_target_pairs={{0,1},{1,0},{2,3},{3,2},{4,5},{5,4},{6,7},{7,6},{8,9},{9,8},{10,11... | collective-permute-start | bytes 7077896 | tf_op jit(solution)/shard_map/ppermute | solution.py:732
  275.0 645.9 %reduce-scatter.9.cloned.1.call-start = ((), (), s32[]{:S(2)}) async-start(), calls=%async_computation.6 | async-start | bytes 13369344 | tf_op jit(solution)/shard_map/reduce_scatter | solution.py:833
  278.0 66.3 %collective-permute-start.8 = (bf16[3,6,256,256]{3,2,1,0:T(8,128)(2,1)}, bf16[3,6,256,256]{3,2,1,0:T(8,128)(2,1)S(1)}, u32[]{:S(2)}, u32[]{:S(2)}) collective-permute-start(bf16[3,6,256,256]{3,2,1,0:T(8,128)(2,1)} %others.5.refs_3_), channel_id=1, source_target_pairs={{0,2},{1,3},{2,0},{3,1},{4,6},{5,7},{6,4},{7,5},{8,10},{9,11},{10,... | collective-permute-start | bytes 7077896 | tf_op jit(solution)/shard_map/ppermute | solution.py:732
  278.1 66.2 %collective-permute-start.7 = (bf16[3,6,256,256]{3,2,1,0:T(8,128)(2,1)}, bf16[3,6,256,256]{3,2,1,0:T(8,128)(2,1)S(1)}, u32[]{:S(2)}, u32[]{:S(2)}) collective-permute-start(bf16[3,6,256,256]{3,2,1,0:T(8,128)(2,1)} %others.5.refs_3_), channel_id=1, source_target_pairs={{0,1},{1,0},{2,3},{3,2},{4,5},{5,4},{6,7},{7,6},{8,9},{9,8},{10,11... | collective-permute-start | bytes 7077896 | tf_op jit(solution)/shard_map/ppermute | solution.py:732
  344.4 4.7 collective-permute-start.9
  414.7 506.2 %reduce-scatter.11.cloned.1.call-start = ((), (), s32[]{:S(2)}) async-start(), calls=%async_computation.7 | async-start | bytes 13369344 | tf_op jit(solution)/shard_map/reduce_scatter | solution.py:833
  417.3 67.1 %collective-permute-start.11 = (bf16[3,6,256,256]{3,2,1,0:T(8,128)(2,1)}, bf16[3,6,256,256]{3,2,1,0:T(8,128)(2,1)}, u32[]{:S(2)}, u32[]{:S(2)}) collective-permute-start(bf16[3,6,256,256]{3,2,1,0:T(8,128)(2,1)} %others.6.refs_3_), channel_id=1, source_target_pairs={{0,2},{1,3},{2,0},{3,1},{4,6},{5,7},{6,4},{7,5},{8,10},{9,11},{10,... | collective-permute-start | bytes 7077896 | tf_op jit(solution)/shard_map/ppermute | solution.py:732
  417.4 69.7 %collective-permute-start.10 = (bf16[3,6,256,256]{3,2,1,0:T(8,128)(2,1)}, bf16[3,6,256,256]{3,2,1,0:T(8,128)(2,1)}, u32[]{:S(2)}, u32[]{:S(2)}) collective-permute-start(bf16[3,6,256,256]{3,2,1,0:T(8,128)(2,1)} %others.6.refs_3_), channel_id=1, source_target_pairs={{0,1},{1,0},{2,3},{3,2},{4,5},{5,4},{6,7},{7,6},{8,9},{9,8},{10,11... | collective-permute-start | bytes 7077896 | tf_op jit(solution)/shard_map/ppermute | solution.py:732
  484.4 4.9 collective-permute-start.12
  487.0 79.3 %collective-permute-start.14 = (bf16[3,6,256,256]{3,2,1,0:T(8,128)(2,1)}, bf16[3,6,256,256]{3,2,1,0:T(8,128)(2,1)}, u32[]{:S(2)}, u32[]{:S(2)}) collective-permute-start(bf16[3,6,256,256]{3,2,1,0:T(8,128)(2,1)} %others.7.refs_3_), channel_id=1, source_target_pairs={{0,2},{1,3},{2,0},{3,1},{4,6},{5,7},{6,4},{7,5},{8,10},{9,11},{10,... | collective-permute-start | bytes 7077896 | tf_op jit(solution)/shard_map/ppermute | solution.py:732
  552.0 424.7 %reduce-scatter.5.cloned.1.call-start = ((), (), s32[]{:S(2)}) async-start(), calls=%async_computation.4 | async-start | bytes 3932160 | tf_op jit(solution)/shard_map/reduce_scatter | solution.py:853
  552.1 20.1 %collective-permute-start.13 = (bf16[3,6,256,256]{3,2,1,0:T(8,128)(2,1)}, bf16[3,6,256,256]{3,2,1,0:T(8,128)(2,1)}, u32[]{:S(2)}, u32[]{:S(2)}) collective-permute-start(bf16[3,6,256,256]{3,2,1,0:T(8,128)(2,1)} %others.7.refs_3_), channel_id=1, source_target_pairs={{0,1},{1,0},{2,3},{3,2},{4,5},{5,4},{6,7},{7,6},{8,9},{9,8},{10,11... | collective-permute-start | bytes 7077896 | tf_op jit(solution)/shard_map/ppermute | solution.py:732
  566.3 5.8 collective-permute-start.15
  691.5 8.8 collective-permute-start.19
  698.1 57.3 %collective-permute-start.23 = (f32[768,16]{1,0:T(8,128)S(1)}, f32[768,16]{1,0:T(8,128)S(1)}, u32[]{:S(2)}, u32[]{:S(2)}) collective-permute-start(f32[768,16]{1,0:T(8,128)S(1)} %slice_add_fusion.2), channel_id=1, source_target_pairs={{0,4},{4,0},{1,5},{5,1},{2,6},{6,2},{3,7},{7,3},{8,12},{12,8},{9,1... | collective-permute-start | bytes 147464 | tf_op jit(solution)/shard_map/ppermute | solution.py:732
  698.2 183.5 %collective-permute-start.21 = (f32[768,1024]{1,0:T(8,128)}, f32[768,1024]{1,0:T(8,128)}, u32[]{:S(2)}, u32[]{:S(2)}) collective-permute-start(f32[768,1024]{1,0:T(8,128)} %get-tuple-element.254), channel_id=1, source_target_pairs={{0,4},{4,0},{1,5},{5,1},{2,6},{6,2},{3,7},{7,3},{8,12},{12,8},{9,1... | collective-permute-start | bytes 9437192 | tf_op jit(solution)/shard_map/ppermute | solution.py:732
  700.2 181.5 %collective-permute-start.22 = (f32[768,1024]{1,0:T(8,128)}, f32[768,1024]{1,0:T(8,128)}, u32[]{:S(2)}, u32[]{:S(2)}) collective-permute-start(f32[768,1024]{1,0:T(8,128)} %get-tuple-element.255), channel_id=1, source_target_pairs={{0,4},{4,0},{1,5},{5,1},{2,6},{6,2},{3,7},{7,3},{8,12},{12,8},{9,1... | collective-permute-start | bytes 9437192 | tf_op jit(solution)/shard_map/ppermute | solution.py:732
  700.3 166.1 %collective-permute-start.18 = (bf16[4,6,256,256]{3,2,1,0:T(8,128)(2,1)}, bf16[4,6,256,256]{3,2,1,0:T(8,128)(2,1)}, u32[]{:S(2)}, u32[]{:S(2)}) collective-permute-start(bf16[4,6,256,256]{3,2,1,0:T(8,128)(2,1)} %get-tuple-element.339), channel_id=1, source_target_pairs={{0,1},{1,0},{2,3},{3,2},{4,5},{5,4},{6,7},{7,6},{8,9},{9,8},{10,11... | collective-permute-start | bytes 9437192 | tf_op jit(solution)/shard_map/ppermute | solution.py:732
  706.0 47.8 %copy-start.10 = (f32[768,128]{1,0:T(8,128)S(1)}, f32[768,128]{1,0:T(8,128)}, u32[]{:S(2)}) copy-start(f32[768,128]{1,0:T(8,128)} %get-tuple-element.246) | copy-start | bytes 1179652
  706.0 160.5 %collective-permute-start.20 = (bf16[4,6,256,256]{3,2,1,0:T(8,128)(2,1)}, bf16[4,6,256,256]{3,2,1,0:T(8,128)(2,1)}, u32[]{:S(2)}, u32[]{:S(2)}) collective-permute-start(bf16[4,6,256,256]{3,2,1,0:T(8,128)(2,1)} %fusion.10), channel_id=1, source_target_pairs={{0,2},{1,3},{2,0},{3,1},{4,6},{5,7},{6,4},{7,5},{8,10},{9,11},{10,... | collective-permute-start | bytes 9437192 | tf_op jit(solution)/shard_map/ppermute | solution.py:732
  753.8 99.2 %copy-start.9 = (f32[1536,128]{1,0:T(8,128)S(1)}, f32[1536,128]{1,0:T(8,128)}, u32[]{:S(2)}) copy-start(f32[1536,128]{1,0:T(8,128)} %get-tuple-element.256) | copy-start | bytes 2359300
  755.4 97.4 %collective-permute-start.24 = (f32[768,16]{1,0:T(8,128)S(1)}, f32[768,16]{1,0:T(8,128)S(1)}, u32[]{:S(2)}, u32[]{:S(2)}) collective-permute-start(f32[768,16]{1,0:T(8,128)S(1)} %slice_add_fusion.1), channel_id=1, source_target_pairs={{0,4},{4,0},{1,5},{5,1},{2,6},{6,2},{3,7},{7,3},{8,12},{12,8},{9,1... | collective-permute-start | bytes 147464 | tf_op jit(solution)/shard_map/ppermute | solution.py:732
  881.8 33.1 %copy-start.45 = (f32[1536]{0:T(1024)S(1)}, f32[1536]{0:T(1024)}, u32[]{:S(2)}) copy-start(f32[1536]{0:T(1024)} %get-tuple-element.362) | copy-start | bytes 18436
  920.8 76.0 %copy-start.51 = (f32[8,128]{1,0:T(8,128)S(1)}, f32[8,128]{1,0:T(8,128)}, u32[]{:S(2)}) copy-start(f32[8,128]{1,0:T(8,128)} %get-tuple-element.258) | copy-start | bytes 12292
  920.8 76.1 %copy-start.36 = (f32[256,128]{1,0:T(8,128)S(1)}, f32[256,128]{1,0:T(8,128)}, u32[]{:S(2)}) copy-start(f32[256,128]{1,0:T(8,128)} %get-tuple-element.261) | copy-start | bytes 393220
  922.8 53.9 %collective-permute-start.30 = (bf16[3,6,256,256]{3,2,1,0:T(8,128)(2,1)S(1)}, bf16[3,6,256,256]{3,2,1,0:T(8,128)(2,1)}, u32[]{:S(2)}, u32[]{:S(2)}) collective-permute-start(bf16[3,6,256,256]{3,2,1,0:T(8,128)(2,1)S(1)} %pad_maximum_fusion.refs_0_), channel_id=1, source_target_pairs={{0,2},{1,3},{2,0},{3,1},{4,6},{5,7},{6,4},{7,5},{8,10},{9,11},{10,... | collective-permute-start | bytes 7077896 | tf_op jit(solution)/shard_map/ppermute | solution.py:732
  923.6 71.3 %collective-permute-start.17 = (f32[768,1024]{1,0:T(8,128)}, f32[768,1024]{1,0:T(8,128)}, u32[]{:S(2)}, u32[]{:S(2)}) collective-permute-start(f32[768,1024]{1,0:T(8,128)} %get-tuple-element.243), channel_id=1, source_target_pairs={{0,4},{4,0},{1,5},{5,1},{2,6},{6,2},{3,7},{7,3},{8,12},{12,8},{9,1... | collective-permute-start | bytes 9437192 | tf_op jit(solution)/shard_map/ppermute | solution.py:732
  924.5 136.8 %collective-permute-start.16 = (f32[768,1024]{1,0:T(8,128)}, f32[768,1024]{1,0:T(8,128)}, u32[]{:S(2)}, u32[]{:S(2)}) collective-permute-start(f32[768,1024]{1,0:T(8,128)} %get-tuple-element.237), channel_id=1, source_target_pairs={{0,4},{4,0},{1,5},{5,1},{2,6},{6,2},{3,7},{7,3},{8,12},{12,8},{9,1... | collective-permute-start | bytes 9437192 | tf_op jit(solution)/shard_map/ppermute | solution.py:732
  925.6 151.7 %collective-permute-start.29 = (bf16[3,6,256,256]{3,2,1,0:T(8,128)(2,1)S(1)}, bf16[3,6,256,256]{3,2,1,0:T(8,128)(2,1)}, u32[]{:S(2)}, u32[]{:S(2)}) collective-permute-start(bf16[3,6,256,256]{3,2,1,0:T(8,128)(2,1)S(1)} %pad_maximum_fusion.refs_0_), channel_id=1, source_target_pairs={{0,1},{1,0},{2,3},{3,2},{4,5},{5,4},{6,7},{7,6},{8,9},{9,8},{10,11... | collective-permute-start | bytes 7077896 | tf_op jit(solution)/shard_map/ppermute | solution.py:732
  976.7 100.6 %collective-permute-start.31 = (bf16[3,6,256,256]{3,2,1,0:T(8,128)(2,1)}, bf16[3,6,256,256]{3,2,1,0:T(8,128)(2,1)}, u32[]{:S(2)}, u32[]{:S(2)}) collective-permute-start(bf16[3,6,256,256]{3,2,1,0:T(8,128)(2,1)} %collective-permute-done.30.refs_2_), channel_id=1, source_target_pairs={{0,1},{1,0},{2,3},{3,2},{4,5},{5,4},{6,7},{7,6},{8,9},{9,8},{10,11... | collective-permute-start | bytes 7077896 | tf_op jit(solution)/shard_map/ppermute | solution.py:732
  976.7 20.2 %collective-permute-start.27 = (bf16[1,6,256,256]{3,2,1,0:T(8,128)(2,1)}, bf16[1,6,256,256]{3,2,1,0:T(8,128)(2,1)S(1)}, u32[]{:S(2)}, u32[]{:S(2)}) collective-permute-start(bf16[1,6,256,256]{3,2,1,0:T(8,128)(2,1)} %reduce-scatter.5.cloned.1.call-done), channel_id=1, source_target_pairs={{0,2},{1,3},{2,0},{3,1},{4,6},{5,7},{6,4},{7,5},{8,10},{9,11},{10,... | collective-permute-start | bytes 2359304 | tf_op jit(solution)/shard_map/ppermute | solution.py:732
  994.9 89.7 %collective-permute-start.26 = (bf16[1,6,256,256]{3,2,1,0:T(8,128)(2,1)}, bf16[1,6,256,256]{3,2,1,0:T(8,128)(2,1)}, u32[]{:S(2)}, u32[]{:S(2)}) collective-permute-start(bf16[1,6,256,256]{3,2,1,0:T(8,128)(2,1)} %reduce-scatter.5.cloned.1.call-done), channel_id=1, source_target_pairs={{0,1},{1,0},{2,3},{3,2},{4,5},{5,4},{6,7},{7,6},{8,9},{9,8},{10,11... | collective-permute-start | bytes 2359304 | tf_op jit(solution)/shard_map/ppermute | solution.py:732
  996.9 87.7 %collective-permute-start.28 = (bf16[1,6,256,256]{3,2,1,0:T(8,128)(2,1)S(1)}, bf16[1,6,256,256]{3,2,1,0:T(8,128)(2,1)}, u32[]{:S(2)}, u32[]{:S(2)}) collective-permute-start(bf16[1,6,256,256]{3,2,1,0:T(8,128)(2,1)S(1)} %collective-permute-done.27.refs_2_), channel_id=1, source_target_pairs={{0,1},{1,0},{2,3},{3,2},{4,5},{5,4},{6,7},{7,6},{8,9},{9,8},{10,11... | collective-permute-start | bytes 2359304 | tf_op jit(solution)/shard_map/ppermute | solution.py:732
  1061.3 11.6 %collective-permute-start.25 = (f32[264,128]{1,0:T(8,128)S(1)}, f32[264,128]{1,0:T(8,128)}, u32[]{:S(2)}, u32[]{:S(2)}) collective-permute-start(f32[264,128]{1,0:T(8,128)S(1)} %constant_dynamic-update-slice_fusion.2), channel_id=1, source_target_pairs={{0,4},{4,0},{1,5},{5,1},{2,6},{6,2},{3,7},{7,3},{8,12},{12,8},{9,1... | collective-permute-start | bytes 405512 | tf_op jit(solution)/shard_map/ppermute | solution.py:732
  (47 other events, 432.0 us)
Sparse Core Ops, SparseCore 0:
  10.7 62.3 all-gather.8
  75.2 62.0 all-gather.10
  138.9 62.0 all-gather.12
  202.4 62.0 all-gather.14
  275.1 140.9 reduce-scatter.6
  420.0 160.2 reduce-scatter.8
  584.4 134.1 reduce-scatter.10
  873.7 68.0 reduce-scatter.4
